TPU v7x, 32 devices: a whole 2x2x4 slice. The times are simulated.
32 devices in a mesh: grp: 2 (over x), dom: 4 (over y, core), pen: 4 (over z).
Axes of the slice: x: 2, y: 2, z: 4, core: 2. Of those that a mesh axis runs over, the one named last changes fastest.
Arguments:
- atoms: float32 [4, 2, 4, 16384], P(None, 'grp', 'dom', 'pen'), may hold values from -6 to 6, as said below
- pair_home: int32 [2, 4, 256], P('grp', 'dom', 'pen'), may hold values from 0 to 31
- pair_other: int32 [2, 4, 256], P('grp', 'dom', 'pen'), may hold values from 0 to 287
Outputs:
- short_forces: float32 [3, 2, 4, 16384], P(None, 'grp', 'dom', 'pen')
- long_forces: float32 [3, 2, 4, 16384], P(None, 'grp', 'dom', 'pen')
Inputs may be any that keep to these rules, and one draw needn't show every extreme that they name: `atoms`: in block (g, d, p) the first coordinate lies in [d / 4, (d + 0.98) / 4), the second in [p / 4, (p + 0.98) / 4), the third in [0, 1); the fourth component is the charge, within -6 to 6.
All inputs are finite; a program needn't handle non-finite values.
Results may differ from a plain program's by a relative error of at most 0.0003.
Values sent between devices are 32-bit elements; how exact they have to be, the bound alone decides.
No kernel may reach another device: no remote copies, remote signals or barrier semaphores. Data moves between devices by JAX's collectives and lax.ppermute only.
A program may use at most 64 MiB of HBM per device.

v0:
```python
import math

import jax
import jax.numpy as jnp
from jax import lax
from jax.sharding import PartitionSpec as P

NG = 128
TILE = 128


exact_precision = lax.Precision.HIGHEST


def with_halo(block, sides, width):
    for axis, dim in sides:
        count = lax.axis_size(axis)
        forward = [(i, i + 1) for i in range(count - 1)]
        forward.append((count - 1, 0))
        backward = [(target, source) for source, target in forward]
        low = lax.ppermute(
            lax.slice_in_dim(block, block.shape[dim] - width, None, axis=dim), axis, forward
        )
        high = lax.ppermute(lax.slice_in_dim(block, 0, width, axis=dim), axis, backward)
        block = jnp.concatenate([low, block, high], axis=dim)
    return block


def passed_along(block, axis, distance):
    devices = range(lax.axis_size(axis))
    route = [((i - distance) % len(devices), i) for i in devices]
    return lax.ppermute(block, axis, route)


def matmul(left, right):
    return jnp.dot(left, right, precision=exact_precision, preferred_element_type=jnp.float32)


def spline_terms(scaled):
    floored = jnp.floor(scaled)
    fraction = scaled - floored
    remain = 1.0 - fraction
    frac_sq = fraction * fraction
    frac_cube = frac_sq * fraction
    thetas = [
        remain * remain * remain / 6.0,
        (3.0 * frac_cube - 6.0 * frac_sq + 4.0) / 6.0,
        (-3.0 * frac_cube + 3.0 * frac_sq + 3.0 * fraction + 1.0) / 6.0,
        frac_cube / 6.0,
    ]
    slopes = [
        -0.5 * remain * remain,
        1.5 * frac_sq - 2.0 * fraction,
        -1.5 * frac_sq + fraction + 0.5,
        0.5 * frac_sq,
    ]
    return (floored.astype(jnp.int32) - 3, thetas, slopes)


def spline_rows(coords, anchor, planes, grid_cells):
    lowest, thetas, slopes = spline_terms(coords * grid_cells)
    plane_ids = lax.broadcasted_iota(jnp.int32, (planes, 1), 0)
    values = jnp.zeros((planes, coords.shape[0]), jnp.float32)
    slopes_out = jnp.zeros_like(values)
    for offset in range(4):
        matches = (jnp.mod(lowest + offset - anchor, grid_cells)[None, :] == plane_ids).astype(
            jnp.float32
        )
        values = values + matches * thetas[offset][None, :]
        slopes_out = slopes_out + matches * slopes[offset][None, :]
    return (values, slopes_out)


def pair_push(home_pos, other_pos, scales):
    displace = home_pos[:, :3, :, None] - other_pos[:, :3, None, :]
    displace = displace - jnp.floor(displace + 0.5)
    scaled = displace * scales[None, :, None, None]
    weight = jnp.exp(-0.5 * jnp.sum(scaled * scaled, axis=1)) * other_pos[:, 3, None, :]
    return jnp.sum(scaled * weight[:, None], axis=3) * home_pos[:, 3:4, :]


def green_factor(freq_x, freq_y, freq_z, grid_cells):

    def signed(frequencies):
        return jnp.where(frequencies < grid_cells // 2, frequencies, frequencies - grid_cells)

    def modulus(frequencies):
        turned = 2.0 * jnp.pi * signed(frequencies).astype(jnp.float32) / grid_cells
        ratio = (2.0 + jnp.cos(turned)) / 3.0
        return 1.0 / (ratio * ratio)

    signed_x = signed(freq_x)
    signed_y = signed(freq_y)
    signed_z = signed(freq_z)
    square = (signed_x * signed_x + signed_y * signed_y + signed_z * signed_z).astype(jnp.float32)
    beta = 0.6 * grid_cells
    safe = jnp.maximum(square, 1.0)
    value = jnp.exp(-jnp.pi * jnp.pi * square / (beta * beta)) / (jnp.pi * safe)
    value = value * modulus(freq_x) * modulus(freq_y) * modulus(freq_z)
    return jnp.where(square > 0.5, value, 0.0)


def phase_tables(frequencies, cell_ids, grid_cells):
    turns = jnp.mod(frequencies[:, None] * cell_ids[None, :], grid_cells).astype(jnp.float32)
    angle = turns * (2.0 * jnp.pi / grid_cells)
    return (jnp.cos(angle), jnp.sin(angle))


def spread_mesh(spread_atoms, first_x, first_y, slab_cells, column, grid_cells):
    span_size = min(1024, spread_atoms.shape[1])
    batches = spread_atoms.reshape(4, -1, span_size).transpose(1, 0, 2)

    def spread_step(totals, atom_batch):
        weight_x, unused_x = spline_rows(atom_batch[0], first_x, slab_cells, grid_cells)
        weight_y, unused_y = spline_rows(atom_batch[1], first_y, column, grid_cells)
        weight_z, unused_z = spline_rows(atom_batch[2], 0, grid_cells, grid_cells)
        weighted_y = weight_y * atom_batch[3][None, :]
        paired = weight_x[:, None, :] * weighted_y[None, :, :]
        paired = paired.reshape(slab_cells * column, span_size)
        product = lax.dot_general(
            paired,
            weight_z,
            (((1,), (1,)), ((), ())),
            precision=exact_precision,
            preferred_element_type=jnp.float32,
        )
        return (totals + product, None)

    totals, unused = lax.scan(
        spread_step, jnp.zeros((slab_cells * column, grid_cells), jnp.float32), batches
    )
    return totals


def forward_lines(cos_tab, sin_tab, real_part, imag_part):
    return (
        matmul(cos_tab, real_part) + matmul(sin_tab, imag_part),
        matmul(cos_tab, imag_part) - matmul(sin_tab, real_part),
    )


def inverse_lines(cos_tab, sin_tab, real_part, imag_part):
    return (
        matmul(cos_tab, real_part) - matmul(sin_tab, imag_part),
        matmul(cos_tab, imag_part) + matmul(sin_tab, real_part),
    )


def on_device(atoms, pair_home, pair_other):
    grid_cells = NG
    groups = lax.axis_size("grp")
    domains = lax.axis_size("dom")
    pencils = lax.axis_size("pen")
    slab_cells = grid_cells // domains
    column = grid_cells // pencils
    atom_count = atoms.shape[3]
    tile_count = atom_count // TILE
    dom_at = lax.axis_index("dom")
    pen_at = lax.axis_index("pen")
    grp_at = lax.axis_index("grp")
    first_x = dom_at * slab_cells
    first_y = pen_at * column
    local_atoms = atoms.reshape(1, 1, 4 * atom_count)
    nearby = with_halo(local_atoms, (("dom", 0), ("pen", 1)), 1)
    nearby = nearby.reshape(3, 3, 4, atom_count)
    tiled = (
        nearby.reshape(9, 4, tile_count, TILE)
        .transpose(0, 2, 1, 3)
        .reshape(9 * tile_count, 4, TILE)
    )
    own_tiles = tiled[4 * tile_count : 5 * tile_count]
    home_ids = pair_home.reshape(-1)
    other_ids = pair_other.reshape(-1)
    pair_count = home_ids.shape[0]
    scales = jnp.array([2.0 * domains, 2.0 * pencils, 2.0 * domains], jnp.float32)

    def pair_group(id_pair):
        home_blk, other_blk = id_pair
        return pair_push(own_tiles[home_blk], tiled[other_blk], scales)

    pushes = lax.map(pair_group, (home_ids.reshape(-1, 16), other_ids.reshape(-1, 16)))
    pushes = pushes.reshape(pair_count, 3 * TILE)
    owners = (home_ids[:, None] == lax.broadcasted_iota(jnp.int32, (1, tile_count), 1)).astype(
        jnp.float32
    )
    summed = lax.dot_general(
        owners,
        pushes,
        (((0,), (0,)), ((), ())),
        precision=exact_precision,
        preferred_element_type=jnp.float32,
    )
    short_out = summed.reshape(tile_count, 3, TILE).transpose(1, 0, 2).reshape(3, 1, 1, atom_count)
    short_out = short_out * (2.0 / math.sqrt(atom_count / domains))
    spread_atoms = nearby[1:3, 1:3].transpose(2, 0, 1, 3).reshape(4, 4 * atom_count)
    z_ids = lax.iota(jnp.int32, grid_cells)
    cos_z, sin_z = phase_tables(z_ids, z_ids, grid_cells)
    charge_mesh = spread_mesh(spread_atoms, first_x, first_y, slab_cells, column, grid_cells)
    kz_rows = grid_cells // groups
    kz_part = kz_rows // domains
    kx_part = grid_cells // pencils
    z_real = matmul(charge_mesh, cos_z)
    z_imag = -matmul(charge_mesh, sin_z)
    sum_real, sum_imag = (
        lax.psum_scatter(z_real, "grp", scatter_dimension=1, tiled=True),
        lax.psum_scatter(z_imag, "grp", scatter_dimension=1, tiled=True),
    )
    sum_real = sum_real.reshape(slab_cells, column, kz_rows)
    sum_imag = sum_imag.reshape(slab_cells, column, kz_rows)
    line_real, line_imag = (
        lax.all_to_all(sum_real, "dom", split_axis=2, concat_axis=0, tiled=True),
        lax.all_to_all(sum_imag, "dom", split_axis=2, concat_axis=0, tiled=True),
    )
    fx_real, fx_imag = forward_lines(
        cos_z,
        sin_z,
        line_real.reshape(grid_cells, column * kz_part),
        line_imag.reshape(grid_cells, column * kz_part),
    )
    fx_real = fx_real.reshape(grid_cells, column, kz_part)
    fx_imag = fx_imag.reshape(grid_cells, column, kz_part)
    ylin_real, ylin_imag = (
        lax.all_to_all(fx_real, "pen", split_axis=0, concat_axis=1, tiled=True),
        lax.all_to_all(fx_imag, "pen", split_axis=0, concat_axis=1, tiled=True),
    )
    ylin_real = ylin_real.transpose(1, 0, 2).reshape(grid_cells, kx_part * kz_part)
    ylin_imag = ylin_imag.transpose(1, 0, 2).reshape(grid_cells, kx_part * kz_part)
    fy_real, fy_imag = forward_lines(cos_z, sin_z, ylin_real, ylin_imag)
    kx_ids = pen_at * kx_part + lax.iota(jnp.int32, kx_part)
    kz_ids = grp_at * kz_rows + dom_at * kz_part + lax.iota(jnp.int32, kz_part)
    factor = green_factor(
        kx_ids[None, :, None], z_ids[:, None, None], kz_ids[None, None, :], grid_cells
    )
    factor = factor.reshape(grid_cells, kx_part * kz_part)
    iy_real, iy_imag = inverse_lines(cos_z, sin_z, fy_real * factor, fy_imag * factor)
    iy_real = iy_real.reshape(grid_cells, kx_part, kz_part).transpose(1, 0, 2)
    iy_imag = iy_imag.reshape(grid_cells, kx_part, kz_part).transpose(1, 0, 2)
    back_real, back_imag = (
        lax.all_to_all(iy_real, "pen", split_axis=1, concat_axis=0, tiled=True),
        lax.all_to_all(iy_imag, "pen", split_axis=1, concat_axis=0, tiled=True),
    )
    ix_real, ix_imag = inverse_lines(
        cos_z,
        sin_z,
        back_real.reshape(grid_cells, column * kz_part),
        back_imag.reshape(grid_cells, column * kz_part),
    )
    ix_real = ix_real.reshape(grid_cells, column, kz_part)
    ix_imag = ix_imag.reshape(grid_cells, column, kz_part)
    slab_real, slab_imag = (
        lax.all_to_all(ix_real, "dom", split_axis=0, concat_axis=2, tiled=True),
        lax.all_to_all(ix_imag, "dom", split_axis=0, concat_axis=2, tiled=True),
    )
    whole_real, whole_imag = (
        lax.all_gather(slab_real, "grp", axis=2, tiled=True),
        lax.all_gather(slab_imag, "grp", axis=2, tiled=True),
    )
    own_pot = matmul(whole_real.reshape(-1, grid_cells), cos_z) - matmul(
        whole_imag.reshape(-1, grid_cells), sin_z
    )
    own_pot = own_pot.reshape(slab_cells, column, grid_cells)
    lower_planes = passed_along(own_pot[slab_cells - 3 :], "dom", 1)
    taller = jnp.concatenate([lower_planes, own_pot], axis=0)
    side_planes = passed_along(taller[:, column - 3 :], "pen", 1)
    rimmed = jnp.concatenate([side_planes, taller], axis=1)
    flat_pot = rimmed.transpose(1, 0, 2).reshape(-1, grid_cells)
    batch_size = min(256, atom_count)
    own_atoms = atoms.reshape(4, -1, batch_size).transpose(1, 0, 2)

    def interpolate(atom_batch):
        weight_x, slope_x = spline_rows(atom_batch[0], first_x - 3, slab_cells + 3, grid_cells)
        weight_y, slope_y = spline_rows(atom_batch[1], first_y - 3, column + 3, grid_cells)
        weight_z, slope_zw = spline_rows(atom_batch[2], 0, grid_cells, grid_cells)
        along_z = matmul(flat_pot, weight_z).reshape(column + 3, slab_cells + 3, batch_size)
        slope_z = matmul(flat_pot, slope_zw).reshape(column + 3, slab_cells + 3, batch_size)
        grad_x = jnp.sum(weight_y[:, None] * slope_x[None] * along_z, axis=(0, 1))
        grad_y = jnp.sum(slope_y[:, None] * weight_x[None] * along_z, axis=(0, 1))
        grad_z = jnp.sum(weight_y[:, None] * weight_x[None] * slope_z, axis=(0, 1))
        return jnp.stack([grad_x, grad_y, grad_z]) * atom_batch[3][None, :]

    gradients = lax.map(interpolate, own_atoms)
    gradients = gradients.transpose(1, 0, 2).reshape(3, 1, 1, atom_count)
    total_atoms = atom_count * groups * domains * pencils
    long_scale = -0.4 * grid_cells / math.sqrt(grid_cells * total_atoms)
    return (short_out, gradients * long_scale)


def solution(mesh):
    placed = (P(None, "grp", "dom", "pen"), P("grp", "dom", "pen"), P("grp", "dom", "pen"))
    return jax.shard_map(
        on_device,
        mesh=mesh,
        in_specs=placed,
        out_specs=(P(None, "grp", "dom", "pen"), P(None, "grp", "dom", "pen")),
        check_vma=False,
    )
```

profile of v0, /device:TPU:0, one launch (start us, length us, event | category | flops | bytes accessed | tf_op | source)
XLA Modules:
  0.0 624.2 jit_solution(14674423635680356168)
XLA Ops:
  9.7 2.7 collective-permute-done.1
  14.6 3.7 collective-permute-start.3
  18.3 5.3 collective-permute-done.3
  23.6 3.2 collective-permute-done.2
  28.7 132.2 %while.44 = (s32[]{:T(128)}, f32[1024,128]{1,0:T(8,128)S(1)}, f32[16,4,1024]{2,1,0:T(4,128)S(1)}, s32[]{:T(128)}, s32[]{:T(128)}, /*index=5*/s32[]{:T(128)}, s32[]{:T(128)}, s32[]{}, s32[]{}, s32[]{}) while((s32[]{:T(128)}, f32[1024,128]{1,0:T(8,128)S(1)}, f32[16,4,1024]{2,1,0:T(4,128)S(1)}, s32[]{:T(128)}, s32[]{:T(128)}, ...), condition=%wide.region_5.6_spmd.clone, body=%wide.region_4.5_spmd.clone.sunk | while | flops 1614345216 | bytes 10219699 | solution.py:129
  31.5 5.5 convolution_add_fusion.6
  39.7 5.5 convolution_add_fusion.6
  48.0 5.5 convolution_add_fusion.6
  56.3 5.5 convolution_add_fusion.6
  64.5 5.5 convolution_add_fusion.6
  72.8 5.5 convolution_add_fusion.6
  81.0 5.5 convolution_add_fusion.6
  89.3 5.5 convolution_add_fusion.6
  97.6 5.5 convolution_add_fusion.6
  105.8 5.5 convolution_add_fusion.6
  114.1 5.5 convolution_add_fusion.6
  122.3 5.5 convolution_add_fusion.6
  130.6 5.5 convolution_add_fusion.6
  138.9 5.5 convolution_add_fusion.6
  147.1 5.5 convolution_add_fusion.6
  155.4 5.5 convolution_add_fusion.6
  165.6 12.0 %reduce-scatter.3.cloned.1.call-done = f32[1024,64]{0,1:T(8,128)} async-done(((f32[1024,128]{0,1:T(8,128)}), f32[1024,64]{0,1:T(8,128)}) %reduce-scatter.3.cloned.1.call-update) | async-done | bytes 262160 | tf_op jit(solution)/shard_map/reduce_scatter | solution.py:205
  180.8 3.4 all-to-all-start
  184.3 10.2 %reduce-scatter.5.cloned.1.call-done = f32[1024,64]{0,1:T(8,128)} async-done(((f32[1024,128]{0,1:T(8,128)}), f32[1024,64]{0,1:T(8,128)}) %reduce-scatter.5.cloned.1.call-update) | async-done | bytes 262160 | tf_op jit(solution)/shard_map/reduce_scatter | solution.py:206
  197.7 4.5 all-to-all-start.1
  216.0 4.7 all-to-all-start.2
  223.9 5.6 all-to-all-done.2
  229.5 4.2 all-to-all-start.3
  255.1 5.3 all-to-all-start.4
  263.5 3.6 all-to-all-done.4
  267.1 3.4 all-to-all-start.5
  283.4 3.4 all-to-all-start.6
  289.3 3.5 all-to-all-done.6
  292.8 3.7 all-to-all-start.7
  298.3 26.2 %all_gather.6 = f32[32,32,128]{1,2,0:T(8,128)S(1)} all-gather(f32[32,32,64]{1,2,0:T(8,128)S(1)} %bitcast.267), channel_id=1, replica_groups=mesh['grp'=2,'dom'=4,'pen'=4] {'grp'}, dimensions={2}, use_global_device_ids=true | all-gather | bytes 786432 | tf_op jit(solution)/shard_map/all_gather | solution.py:255
  327.9 25.5 %all_gather.7 = f32[32,32,128]{1,2,0:T(8,128)S(1)} all-gather(f32[32,32,64]{1,2,0:T(8,128)S(1)} %bitcast.268), channel_id=1, replica_groups=mesh['grp'=2,'dom'=4,'pen'=4] {'grp'}, dimensions={2}, use_global_device_ids=true | all-gather | bytes 786432 | tf_op jit(solution)/shard_map/all_gather | solution.py:256
  354.8 24.9 %while.43 = (s32[]{:T(128)}, f32[4,16,3,128]{3,2,1,0:T(4,128)S(1)}, s32[4,16]{1,0:T(4,128)}, f32[32,4,128]{2,1,0:T(4,128)S(1)}, s32[4,16]{1,0:T(4,128)}, /*index=5*/f32[288,4,128]{2,1,0:T(4,128)}, s32[]{:T(128)}) while((s32[]{:T(128)}, f32[4,16,3,128]{3,2,1,0:T(4,128)S(1)}, s32[4,16]{1,0:T(4,128)}, ...), condition=%wide.region_3.4_spmd.clone, body=%wide.region_0.3_spmd.sunk.clone.sunk | while | flops 10750050 | bytes 4571741 | solution.py:181
  382.1 4.3 collective-permute-done.5
  386.6 228.7 %while.42 = (s32[]{:T(128)}, f32[16,3,256]{2,1,0:T(4,128)}, f32[16,4,256]{2,0,1:T(8,128)}, s32[]{:T(128)}, s32[]{:T(128)}, /*index=5*/f32[1225,128]{1,0:T(8,128)...) while((s32[]{:T(128)}, f32[16,3,256]{2,1,0:T(4,128)}, f32[16,4,256]{2,0,1:T(8,128)}, s32[]{:T(128)}, ...), condition=%wide.region_12.13_spmd, body=%wide.region_8.12_spmd.sunk | while | flops 967310080 | bytes 21715156 | solution.py:281
  397.1 2.6 multiply_reduce_fusion.3
  403.3 2.5 mul.3542
  411.4 2.6 multiply_reduce_fusion.3
  417.6 2.5 mul.3542
  420.2 2.5 fusion.297
  425.7 2.6 multiply_reduce_fusion.3
  439.9 2.6 multiply_reduce_fusion.3
  448.8 2.5 fusion.297
  454.2 2.6 multiply_reduce_fusion.3
  468.5 2.6 multiply_reduce_fusion.3
  477.3 2.5 fusion.297
  482.8 2.6 multiply_reduce_fusion.3
  491.6 2.5 fusion.297
  497.1 2.6 multiply_reduce_fusion.3
  505.9 2.5 fusion.297
  511.4 2.6 multiply_reduce_fusion.3
  525.7 2.6 multiply_reduce_fusion.3
  540.0 2.6 multiply_reduce_fusion.3
  554.3 2.6 multiply_reduce_fusion.3
  568.6 2.6 multiply_reduce_fusion.3
  577.4 2.5 fusion.297
  582.9 2.6 multiply_reduce_fusion.3
  591.7 2.5 fusion.297
  597.2 2.6 multiply_reduce_fusion.3
  611.5 2.6 multiply_reduce_fusion.3
  (609 shorter events, 316.5 us)
Async XLA Ops:
  7.2 170.4 %reduce-scatter.3.cloned.1.call-start = ((), (), s32[]{:S(2)}) async-start(), calls=%async_computation.10 | async-start | bytes 786432 | tf_op jit(solution)/shard_map/reduce_scatter | solution.py:205
  7.2 5.2 collective-permute-start.1
  9.7 3.9 collective-permute-start
  14.6 8.9 %collective-permute-start.3 = (f32[3,1,16384]{2,1,0:T(1,128)S(1)}, f32[3,1,16384]{2,1,0:T(1,128)S(1)}, u32[]{:S(2)}, u32[]{:S(2)}) collective-permute-start(f32[3,1,16384]{2,1,0:T(1,128)S(1)} %pad_maximum_fusion.1), channel_id=1, source_target_pairs={{1,0},{2,1},{3,2},{0,3},{5,4},{6,5},{7,6},{4,7},{9,8},{10,9},{11,1... | collective-permute-start | bytes 589832 | tf_op jit(solution)/shard_map/ppermute | solution.py:24
  18.3 8.5 %collective-permute-start.2 = (f32[3,1,16384]{2,1,0:T(1,128)S(1)}, f32[3,1,16384]{2,1,0:T(1,128)S(1)}, u32[]{:S(2)}, u32[]{:S(2)}) collective-permute-start(f32[3,1,16384]{2,1,0:T(1,128)S(1)} %pad_maximum_fusion.1), channel_id=1, source_target_pairs={{0,1},{1,2},{2,3},{3,0},{4,5},{5,6},{6,7},{7,4},{8,9},{9,10},{10,1... | collective-permute-start | bytes 589832 | tf_op jit(solution)/shard_map/ppermute | solution.py:21
  162.6 31.9 %reduce-scatter.5.cloned.1.call-start = ((), (), s32[]{:S(2)}) async-start(), calls=%async_computation.11 | async-start | bytes 786432 | tf_op jit(solution)/shard_map/reduce_scatter | solution.py:206
  180.8 16.9 %all-to-all-start = ((f32[4,1,16384]{2,1,0:T(1,128)}), f32[4,1,16384]{2,1,0:T(1,128)S(1)}, u32[]{:S(2)}, u32[]{:S(2)}) async-start(f32[4,1,16384]{2,1,0:T(1,128)} %reshape.2132), calls=%async_computation.1 | async-start | bytes 524288 | tf_op jit(solution)/shard_map/all_to_all | solution.py:211
  197.7 10.6 %all-to-all-start.1 = ((f32[4,1,16384]{2,1,0:T(1,128)}), f32[4,1,16384]{2,1,0:T(1,128)}, u32[]{:S(2)}, u32[]{:S(2)}) async-start(f32[4,1,16384]{2,1,0:T(1,128)} %reshape.2134), calls=%async_computation.3 | async-start | bytes 524288 | tf_op jit(solution)/shard_map/all_to_all | solution.py:212
  214.8 18.9 %copy-start.2 = (f32[4,1,1,4096]{3,2,1,0:T(1,128)S(1)}, f32[4,1,1,4096]{3,2,1,0:T(1,128)}, u32[]{:S(2)}) copy-start(f32[4,1,1,4096]{3,2,1,0:T(1,128)} %param.10) | copy-start | bytes 196612
  216.0 18.5 %copy-start.7 = (s32[1,1,64]{2,1,0:T(1,128)S(1)}, s32[1,1,64]{2,1,0:T(1,128)}, u32[]{:S(2)}) copy-start(s32[1,1,64]{2,1,0:T(1,128)} %param.11) | copy-start | bytes 772
  216.0 19.8 %copy-start.11 = (s32[1,1,64]{2,1,0:T(1,128)S(1)}, s32[1,1,64]{2,1,0:T(1,128)}, u32[]{:S(2)}) copy-start(s32[1,1,64]{2,1,0:T(1,128)} %param.12) | copy-start | bytes 772
  216.0 21.8 %copy-start.10 = (f32[16]{0:T(128)S(1)}, f32[16]{0:T(128)}, u32[]{:S(2)}) copy-start(f32[16]{0:T(128)} %multiply_divide_fusion) | copy-start | bytes 196
  216.0 22.4 %copy-start.9 = (f32[32]{0:T(128)S(1)}, f32[32]{0:T(128)}, u32[]{:S(2)}) copy-start(f32[32]{0:T(128)} %multiply_divide_fusion.2) | copy-start | bytes 388
  216.0 13.5 %all-to-all-start.2 = ((f32[4,1,16384]{2,1,0:T(1,128)}), f32[4,1,16384]{2,1,0:T(1,128)S(1)}, u32[]{:S(2)}, u32[]{:S(2)}) async-start(f32[4,1,16384]{2,1,0:T(1,128)} %reshape.2136), calls=%async_computation.4 | async-start | bytes 524288 | tf_op jit(solution)/shard_map/all_to_all | solution.py:223
  229.5 15.4 %all-to-all-start.3 = ((f32[4,1,16384]{2,1,0:T(1,128)}), f32[4,1,16384]{2,1,0:T(1,128)}, u32[]{:S(2)}, u32[]{:S(2)}) async-start(f32[4,1,16384]{2,1,0:T(1,128)} %reshape.2138), calls=%async_computation.5 | async-start | bytes 524288 | tf_op jit(solution)/shard_map/all_to_all | solution.py:224
  243.6 5.9 copy-start.5
  243.6 5.9 copy-start.6
  248.3 3.6 copy-start.3
  255.1 12.0 %all-to-all-start.4 = ((f32[4,1,16384]{2,1,0:T(1,128)}), f32[4,1,16384]{2,1,0:T(1,128)S(1)}, u32[]{:S(2)}, u32[]{:S(2)}) async-start(f32[4,1,16384]{2,1,0:T(1,128)} %reshape.2140), calls=%async_computation.6 | async-start | bytes 524288 | tf_op jit(solution)/shard_map/all_to_all | solution.py:239
  267.1 10.2 %all-to-all-start.5 = ((f32[4,1,16384]{2,1,0:T(1,128)}), f32[4,1,16384]{2,1,0:T(1,128)S(1)}, u32[]{:S(2)}, u32[]{:S(2)}) async-start(f32[4,1,16384]{2,1,0:T(1,128)} %reshape.2142), calls=%async_computation.7 | async-start | bytes 524288 | tf_op jit(solution)/shard_map/all_to_all | solution.py:240
  283.4 9.4 %all-to-all-start.6 = ((f32[4,1,16384]{2,1,0:T(1,128)}), f32[4,1,16384]{2,1,0:T(1,128)S(1)}, u32[]{:S(2)}, u32[]{:S(2)}) async-start(f32[4,1,16384]{2,1,0:T(1,128)} %reshape.2144), calls=%async_computation.8 | async-start | bytes 524288 | tf_op jit(solution)/shard_map/all_to_all | solution.py:251
  292.8 33.2 %all-to-all-start.7 = ((f32[4,1,16384]{2,1,0:T(1,128)}), f32[4,1,16384]{2,1,0:T(1,128)S(1)}, u32[]{:S(2)}, u32[]{:S(2)}) async-start(f32[4,1,16384]{2,1,0:T(1,128)} %reshape.2146), calls=%async_computation.9 | async-start | bytes 524288 | tf_op jit(solution)/shard_map/all_to_all | solution.py:252
  327.8 27.0 %copy-start.1 = (f32[32,4,128]{2,1,0:T(4,128)S(1)}, f32[32,4,128]{2,1,0:T(4,128)}, u32[]{:S(2)}) copy-start(f32[32,4,128]{2,1,0:T(4,128)} %copy.136) | copy-start | bytes 196612
  327.8 27.0 %copy-start.4 = (f32[4,16,3,128]{3,2,1,0:T(4,128)S(1)}, f32[4,16,3,128]{3,2,1,0:T(4,128)}, u32[]{:S(2)}) copy-start(f32[4,16,3,128]{3,2,1,0:T(4,128)} %custom-call.6) | copy-start | bytes 294916
  354.7 25.0 %collective-permute-start.4 = (f32[3,32,128]{2,1,0:T(8,128)S(1)}, f32[3,32,128]{2,1,0:T(8,128)S(1)}, u32[]{:S(2)}, u32[]{:S(2)}) collective-permute-start(f32[3,32,128]{2,1,0:T(8,128)S(1)} %bitcast.326), channel_id=1, source_target_pairs={{12,0},{0,4},{4,8},{8,12},{13,1},{1,5},{5,9},{9,13},{14,2},{2,6},{... | collective-permute-start | bytes 147464 | tf_op jit(solution)/shard_map/ppermute | solution.py:32
  354.8 26.5 %copy-start.8 = (s32[1,1,64]{2,1,0:T(1,128)S(1)}, s32[1,1,64]{2,1,0:T(1,128)}, u32[]{:S(2)}) copy-start(s32[1,1,64]{2,1,0:T(1,128)} %param.11) | copy-start | bytes 772
  379.8 6.6 %collective-permute-start.5 = (f32[35,3,128]{2,1,0:T(4,128)S(1)}, f32[35,3,128]{2,1,0:T(4,128)S(1)}, u32[]{:S(2)}, u32[]{:S(2)}) collective-permute-start(f32[35,3,128]{2,1,0:T(4,128)S(1)} %pad_maximum_fusion.2), channel_id=1, source_target_pairs={{3,0},{0,1},{1,2},{2,3},{7,4},{4,5},{5,6},{6,7},{11,8},{8,9},{9,10... | collective-permute-start | bytes 161288 | tf_op jit(solution)/shard_map/ppermute | solution.py:32
  395.3 1.8 copy-start
  409.6 1.8 copy-start
  423.9 1.8 copy-start
  438.2 1.8 copy-start
  452.5 1.8 copy-start
  466.8 1.8 copy-start
  481.1 1.8 copy-start
  495.4 1.8 copy-start
  509.7 1.8 copy-start
  524.0 1.8 copy-start
  538.2 1.8 copy-start
  552.5 1.8 copy-start
  566.8 1.8 copy-start
  581.1 1.8 copy-start
  595.4 1.8 copy-start
  609.7 1.8 copy-start
Sparse Core Ops, SparseCore 0:
  162.7 14.7 reduce-scatter.2
  179.8 14.6 reduce-scatter.4
where the time goes:
time: 636 us; the launch traced here: 624 us
  matrix products  189 us (30%)
  local copies, waits for them, and re-layouts  147 us (23%)
  other arithmetic  125 us (20%)
  waiting for transfers between devices  53.7 us (8%)
  blocking collectives  51.7 us (8%)
  starting transfers between devices  40.4 us (6%)
  between operations  15.3 us (2%)
    dot_general x52, matrix products, matmul(): jnp.dot(left, right, precision=exact_precision, preferred_element_type=jn...  100 us
    dot_general x16, matrix products, spread_step(): lax.dot_general(paired, weight_z, (((1,), (1,)), ((), ())), precision=exa...  88.1 us
    mul x16, local copies, waits for them, and re-layouts, interpolate(): grad_z = jnp.sum(weight_y[:, None] * weight_x[None] * slope_z, axis=(0, 1))  40.2 us
    mul x16, other arithmetic, spread_step(): paired = weight_x[:, None, :] * weighted_y[None, :, :]  39.5 us
    all_gather x1, blocking collectives, on_device(): lax.all_gather(slab_real, 'grp', axis=2, tiled=True)  26.2 us
    all_gather x1, blocking collectives, on_device(): lax.all_gather(slab_imag, 'grp', axis=2, tiled=True)  25.5 us
    mul x16, other arithmetic, interpolate(): grad_y = jnp.sum(slope_y[:, None] * weight_x[None] * along_z, axis=(0, 1))  23.8 us
    mul x16, local copies, waits for them, and re-layouts, interpolate(): grad_y = jnp.sum(slope_y[:, None] * weight_x[None] * along_z, axis=(0, 1))  19.7 us
  transfers between devices with their start and end apart: 16, of which 12 were waited for; matrix products, arithmetic and copies ran while one was open for 11% of the time, Pallas kernels for 0%

commit v1 on v0

--- a/solution.py
+++ b/solution.py
@@ -2,7 +2,10 @@
 
 import jax
 import jax.numpy as jnp
+import numpy as np
 from jax import lax
+from jax.experimental import pallas as pl
+from jax.experimental.pallas import tpu as pltpu
 from jax.sharding import PartitionSpec as P
 
 NG = 128
@@ -285,10 +288,477 @@
     return (short_out, gradients * long_scale)
 
 
+LANES = 128
+SUBLANES = 8
+MESH_AXES = ("pen", "grp", "dom")
+
+
+def fast_sizes(groups, domains, pencils, atom_count):
+    devices = groups * domains * pencils
+    if NG != LANES or NG % devices or NG // domains != 32 or NG // pencils != 32:
+        return None
+    share = NG // devices
+    if (domains * share) % SUBLANES or atom_count % 512 or TILE != LANES:
+        return None
+    slab = NG // domains
+    column = NG // pencils
+    return dict(
+        share=share,
+        slab=slab,
+        stride=column + 4,
+        column=column,
+        rows=-(-(slab + 3) * (column + 4) // LANES) * LANES,
+        block=domains * share,
+        groups=groups,
+        domains=domains,
+        pencils=pencils,
+    )
+
+
+def real_basis():
+    freq = np.arange(NG)
+    freq = np.where(freq <= NG // 2, freq, freq - NG // 2)
+    turns = (freq[:, None] * np.arange(NG)[None, :]) % NG
+    angle = turns * (2.0 * np.pi / NG)
+    use_cos = (np.arange(NG) <= NG // 2)[:, None]
+    return freq, np.where(use_cos, np.cos(angle), np.sin(angle)).astype(np.float32)
+
+
+def line_factor(freq):
+    beta = 0.6 * NG
+    ratio = (2.0 + np.cos(2.0 * np.pi * freq / NG)) / 3.0
+    count = np.where((freq == 0) | (freq == NG // 2), 1.0, 2.0)
+    return count * np.exp(-np.pi * np.pi * freq * freq / (beta * beta)) / (ratio * ratio)
+
+
+def split_bf16(value):
+    high = value.astype(jnp.bfloat16)
+    low = (value - high.astype(jnp.float32)).astype(jnp.bfloat16)
+    return high, low
+
+
+def choose(place, options):
+    out = jnp.where(place == 0.0, options[0], 0.0)
+    for k in range(1, 4):
+        out = jnp.where(place == float(k), options[k], out)
+    return out
+
+
+def row_ids(count, lanes):
+    return lax.broadcasted_iota(jnp.int32, (count, lanes), 0).astype(jnp.float32)
+
+
+def spline_parts(coord):
+    scaled = coord * float(NG)
+    floored = jnp.floor(scaled)
+    fraction = scaled - floored
+    remain = 1.0 - fraction
+    frac_sq = fraction * fraction
+    frac_cube = frac_sq * fraction
+    sixth = 1.0 / 6.0
+    thetas = [
+        remain * remain * remain * sixth,
+        (3.0 * frac_cube - 6.0 * frac_sq + 4.0) * sixth,
+        (-3.0 * frac_cube + 3.0 * frac_sq + 3.0 * fraction + 1.0) * sixth,
+        frac_cube * sixth,
+    ]
+    slopes = [
+        -0.5 * remain * remain,
+        1.5 * frac_sq - 2.0 * fraction,
+        -1.5 * frac_sq + fraction + 0.5,
+        0.5 * frac_sq,
+    ]
+    return floored, thetas, slopes
+
+
+def z_place(floored, lanes):
+    place = row_ids(NG, lanes) - floored + 3.0
+    return jnp.where(place >= float(NG), place - float(NG), place)
+
+
+def spread_kernel(first_ref, basis_ref, atoms_ref, out_ref, acc_ref, high_ref, low_ref, *, sizes):
+    step = pl.program_id(0)
+    lanes = atoms_ref.shape[1]
+    rows, stride = sizes["rows"], sizes["stride"]
+    floor_x, theta_x, _ = spline_parts(atoms_ref[0:1, :])
+    floor_y, theta_y, _ = spline_parts(atoms_ref[1:2, :])
+    floor_z, theta_z, _ = spline_parts(atoms_ref[2:3, :])
+    floor_x = floor_x - first_ref[0].astype(jnp.float32)
+    floor_y = floor_y - first_ref[1].astype(jnp.float32)
+    weight_x = choose(row_ids(stride + 4, lanes) - floor_x, theta_x)
+    period = row_ids(2 * stride, lanes)
+    period = jnp.where(period >= float(stride), period - float(stride), period)
+    weight_y = choose(period - floor_y, theta_y) * atoms_ref[3:4, :]
+    weight_z = choose(z_place(floor_z, lanes), theta_z)
+    z_high, z_low = split_bf16(weight_z)
+    low_half = lax.broadcasted_iota(jnp.int32, (SUBLANES, lanes), 0) < stride % SUBLANES
+    whole = stride // SUBLANES * SUBLANES
+    for group in range(-(-rows // (4 * stride))):
+        pieces = []
+        for pair in range(2):
+            at = 4 * group + 2 * pair
+            if at >= sizes["slab"] + 4:
+                continue
+            first = jnp.broadcast_to(weight_x[at : at + 1, :], (SUBLANES, lanes))
+            second = jnp.broadcast_to(weight_x[at + 1 : at + 2, :], (SUBLANES, lanes))
+            mixed = jnp.where(low_half, first, second)
+            for tile in range(2 * stride // SUBLANES):
+                factor = first if tile < whole // SUBLANES else second
+                factor = mixed if tile == whole // SUBLANES else factor
+                pieces.append(factor * weight_y[tile * SUBLANES : (tile + 1) * SUBLANES, :])
+        start = group * 4 * stride
+        count = min(4 * stride, rows - start)
+        paired = jnp.concatenate(pieces, axis=0)[:count]
+        high, low = split_bf16(paired)
+        high_ref[start : start + count, :] = high
+        low_ref[start : start + count, :] = low
+    contract = (((1,), (1,)), ((), ()))
+    both = jnp.concatenate([z_high, z_low], axis=0)
+    main = lax.dot_general(high_ref[...], both, contract, preferred_element_type=jnp.float32)
+    rest = lax.dot_general(low_ref[...], z_high, contract, preferred_element_type=jnp.float32)
+    total = main[:, :NG] + main[:, NG:] + rest
+
+    @pl.when(step == 0)
+    def _():
+        acc_ref[...] = total
+
+    @pl.when(step > 0)
+    def _():
+        acc_ref[...] += total
+
+    @pl.when(step == pl.num_programs(0) - 1)
+    def _():
+        out_ref[...] = lax.dot_general(
+            basis_ref[...],
+            acc_ref[...],
+            contract,
+            precision=exact_precision,
+            preferred_element_type=jnp.float32,
+        )
+
+
+def ring_mask(lane, start, length):
+    start = start % LANES
+    if start + length <= LANES:
+        return (lane >= start) & (lane < start + length)
+    return (lane >= start) | (lane < start + length - LANES)
+
+
+def spectral_kernel(
+    line_ref, square_ref, basis_ref, mixed_ref, mixed_t_ref, plane_ref, plane_sq_ref,
+    in_ref, out_ref, sum_ref, work_ref, *, sizes
+):
+    block, share, stride = sizes["block"], sizes["share"], sizes["stride"]
+    slab, column, groups = sizes["slab"], sizes["column"], sizes["groups"]
+    pencils, rows = sizes["pencils"], sizes["rows"]
+    for pen in range(pencils):
+        total = in_ref[pen * groups * block : (pen * groups + 1) * block, :]
+        for grp in range(1, groups):
+            start = (pen * groups + grp) * block
+            total = total + in_ref[start : start + block, :]
+        sum_ref[pen * block : (pen + 1) * block, :] = total
+    lane = lax.broadcasted_iota(jnp.int32, (block, LANES), 1)
+    width = column + 3
+
+    def gathered(x):
+        total = None
+        for pen in range(pencils):
+            shift = (column * pen - 3 - stride * x) % LANES
+            for tile in range(stride * x // LANES, (stride * x + width - 1) // LANES + 1):
+                low = max(0, tile * LANES - stride * x)
+                high = min(width, (tile + 1) * LANES - stride * x)
+                part = sum_ref[pen * block : (pen + 1) * block, tile * LANES : (tile + 1) * LANES]
+                part = pltpu.roll(part, shift, 1) if shift else part
+                mask = ring_mask(lane, column * pen - 3 + low, high - low)
+                part = jnp.where(mask, part, 0.0)
+                total = part if total is None else total + part
+        return total
+
+    for x in range(slab):
+        value = gathered(x + 3)
+        if x >= slab - 3:
+            value = value + pltpu.roll(gathered(x + 3 - slab), block - share, 0)
+        work_ref[x * block : (x + 1) * block, :] = value
+
+    def dot(left, right, contract=(1, 0)):
+        return lax.dot_general(
+            left,
+            right,
+            (((contract[0],), (contract[1],)), ((), ())),
+            precision=exact_precision,
+            preferred_element_type=jnp.float32,
+        )
+
+    work_ref[...] = dot(work_ref[...], basis_ref[...], (1, 1))
+    for kz in range(share):
+        picked = work_ref[pl.ds(kz, NG, stride=share), :]
+        spectrum = dot(mixed_ref[...], picked)
+        square = plane_sq_ref[...] + square_ref[kz]
+        factor = plane_ref[...] * line_ref[kz] / jnp.maximum(square, 1.0)
+        factor = jnp.where(square > 0.5, factor, 0.0)
+        work_ref[pl.ds(kz, NG, stride=share), :] = dot(mixed_t_ref[...], spectrum * factor)
+    work_ref[...] = dot(work_ref[...], basis_ref[...])
+
+    for pen in range(pencils):
+        for tile in range(rows // LANES):
+            total = jnp.zeros((block, LANES), jnp.float32)
+            for x in range(slab + 3):
+                low = max(stride * x, tile * LANES)
+                high = min(stride * x + width, (tile + 1) * LANES)
+                if low >= high:
+                    continue
+                if x >= 3:
+                    value = work_ref[(x - 3) * block : (x - 2) * block, :]
+                else:
+                    value = work_ref[(slab - 3 + x) * block : (slab - 2 + x) * block, :]
+                    value = pltpu.roll(value, share, 0)
+                shift = (stride * x - column * pen + 3) % LANES
+                value = pltpu.roll(value, shift, 1) if shift else value
+                mask = ring_mask(lane, low - tile * LANES, high - low)
+                total = jnp.where(mask, value, total)
+            for grp in range(groups):
+                start = (pen * groups + grp) * block
+                out_ref[start : start + block, tile * LANES : (tile + 1) * LANES] = total
+
+
+def interpolate_kernel(
+    first_ref, basis_ref, coef_ref, atoms_ref, out_ref, pot_ref, along_ref, *, sizes, scale
+):
+    lanes = atoms_ref.shape[1]
+    rows, stride = sizes["rows"], sizes["stride"]
+
+    @pl.when(pl.program_id(0) == 0)
+    def _():
+        potential = lax.dot_general(
+            coef_ref[...],
+            basis_ref[...],
+            (((0,), (0,)), ((), ())),
+            precision=exact_precision,
+            preferred_element_type=jnp.float32,
+        )
+        high, low = split_bf16(potential)
+        pot_ref[:, :NG] = high
+        pot_ref[:, NG : 2 * NG] = low
+        pot_ref[:, 2 * NG :] = high
+
+    floor_x, theta_x, slope_x = spline_parts(atoms_ref[0:1, :])
+    floor_y, theta_y, slope_y = spline_parts(atoms_ref[1:2, :])
+    floor_z, theta_z, slope_z = spline_parts(atoms_ref[2:3, :])
+    floor_x = floor_x - first_ref[0].astype(jnp.float32)
+    floor_y = floor_y - first_ref[1].astype(jnp.float32)
+    place = z_place(floor_z, lanes)
+    columns = []
+    for options in (theta_z, slope_z):
+        high, low = split_bf16(choose(place, options))
+        columns.append(jnp.concatenate([high, high, low], axis=0))
+    along_ref[...] = jnp.dot(
+        pot_ref[...], jnp.concatenate(columns, axis=1), preferred_element_type=jnp.float32
+    )
+    place = row_ids(stride + 4, lanes) - floor_x
+    weight_x, deriv_x = choose(place, theta_x), choose(place, slope_x)
+    period = row_ids(2 * stride, lanes)
+    period = jnp.where(period >= float(stride), period - float(stride), period)
+    place = period - floor_y
+    weight_y, deriv_y = choose(place, theta_y), choose(place, slope_y)
+    low_half = lax.broadcasted_iota(jnp.int32, (SUBLANES, lanes), 0) < stride % SUBLANES
+    middle = stride // SUBLANES
+    grads = [jnp.zeros((SUBLANES, lanes), jnp.float32) for axis in range(3)]
+    for at in range(0, sizes["slab"] + 3, 2):
+        sums = [[None] * 3 for axis in range(3)]
+        for tile in range(2 * stride // SUBLANES):
+            row = at * stride + tile * SUBLANES
+            if row >= rows:
+                continue
+            span = slice(tile * SUBLANES, (tile + 1) * SUBLANES)
+            along = along_ref[row : row + SUBLANES, :lanes]
+            slope = along_ref[row : row + SUBLANES, lanes:]
+            kind = 0 if tile < middle else 1 if tile == middle else 2
+            terms = (along * weight_y[span, :], along * deriv_y[span, :], slope * weight_y[span, :])
+            for axis in range(3):
+                held = sums[axis][kind]
+                sums[axis][kind] = terms[axis] if held is None else held + terms[axis]
+        for axis, table in enumerate((deriv_x, weight_x, weight_x)):
+            first = jnp.broadcast_to(table[at : at + 1, :], (SUBLANES, lanes))
+            second = jnp.broadcast_to(table[at + 1 : at + 2, :], (SUBLANES, lanes))
+            factors = (first, jnp.where(low_half, first, second), second)
+            for kind in range(3):
+                grads[axis] = grads[axis] + sums[axis][kind] * factors[kind]
+    charge = atoms_ref[3:4, :] * scale
+    for axis in range(3):
+        out_ref[axis : axis + 1, :] = jnp.sum(grads[axis], axis=0, keepdims=True) * charge
+
+
+def pair_kernel(home_ref, other_ref, wrap_ref, near_ref, out_ref, *, factors, scale):
+    tiles = near_ref.shape[2] // TILE
+    out_ref[...] = jnp.zeros_like(out_ref)
+    centre = near_ref.shape[0] // 2
+
+    def one_pair(n, carry):
+        home = home_ref[n]
+        other = other_ref[n]
+        around = other // tiles
+        home_at = pl.ds(pl.multiple_of(home * TILE, TILE), TILE)
+        other_at = pl.ds(pl.multiple_of((other - around * tiles) * TILE, TILE), TILE)
+        mine = near_ref[centre, :, home_at]
+        theirs = near_ref[around, :, other_at]
+        turned = jnp.concatenate([theirs, theirs], axis=0).T
+        delta_x = (mine[0:1, :] - wrap_ref[0, around]) - turned[:, 0:1]
+        delta_y = (mine[1:2, :] - wrap_ref[1, around]) - turned[:, 1:2]
+        delta_z = mine[2:3, :] - turned[:, 2:3]
+        delta_z = delta_z - jnp.floor(delta_z + 0.5)
+        scaled = (delta_x * factors[0], delta_y * factors[1], delta_z * factors[2])
+        square = scaled[0] * scaled[0] + scaled[1] * scaled[1] + scaled[2] * scaled[2]
+        weight = jnp.exp(-0.5 * square) * turned[:, 3:4]
+        charge = mine[3:4, :] * scale
+        for axis in range(3):
+            push = jnp.sum(scaled[axis] * weight, axis=0, keepdims=True) * charge
+            out_ref[axis : axis + 1, home_at] += push
+        return carry
+
+    lax.fori_loop(0, home_ref.shape[0], one_pair, 0)
+
+
+def neighbours(block, domains, pencils):
+    found = []
+    for step_dom in (-1, 0, 1):
+        for step_pen in (-1, 0, 1):
+            if step_dom == 0 and step_pen == 0:
+                found.append(block)
+                continue
+            route = [
+                ((dom + step_dom) % domains * pencils + (pen + step_pen) % pencils, dom * pencils + pen)
+                for dom in range(domains)
+                for pen in range(pencils)
+            ]
+            found.append(lax.ppermute(block, ("dom", "pen"), route))
+    return jnp.stack(found)
+
+
+def whole_spec(shape):
+    return pl.BlockSpec(shape, lambda *unused: (0,) * len(shape))
+
+
+def smem_spec():
+    return pl.BlockSpec(memory_space=pltpu.SMEM)
+
+
+def fast_on_device(atoms, pair_home, pair_other, *, sizes):
+    groups, domains, pencils = sizes["groups"], sizes["domains"], sizes["pencils"]
+    rows, share, block = sizes["rows"], sizes["share"], sizes["block"]
+    slab, column, stride = sizes["slab"], sizes["column"], sizes["stride"]
+    devices = groups * domains * pencils
+    atom_count = atoms.shape[3]
+    own = atoms.reshape(4, atom_count)
+    dom_at = lax.axis_index("dom")
+    pen_at = lax.axis_index("pen")
+    grp_at = lax.axis_index("grp")
+    first = jnp.stack([dom_at * slab, pen_at * column]).astype(jnp.int32)
+    freq, basis = real_basis()
+    order = (np.arange(domains)[None, :] * slab + np.arange(slab)[:, None]).reshape(-1)
+    mixed = np.ascontiguousarray(basis[:, order])
+    line = line_factor(freq)
+    plane = jnp.asarray((line[:, None] * line[None, :] / np.pi).astype(np.float32))
+    plane_sq = jnp.asarray((freq[:, None] ** 2 + freq[None, :] ** 2).astype(np.float32))
+    basis_arr = jnp.asarray(basis)
+
+    chunk = 512
+    parallel = pltpu.CompilerParams(dimension_semantics=("arbitrary",))
+    charge = pl.pallas_call(
+        lambda *refs: spread_kernel(*refs, sizes=sizes),
+        grid=(atom_count // chunk,),
+        in_specs=[
+            smem_spec(),
+            whole_spec((NG, NG)),
+            pl.BlockSpec((4, chunk), lambda i: (0, i)),
+        ],
+        out_specs=whole_spec((NG, rows)),
+        out_shape=jax.ShapeDtypeStruct((NG, rows), jnp.float32),
+        scratch_shapes=[
+            pltpu.VMEM((rows, NG), jnp.float32),
+            pltpu.VMEM((rows, chunk), jnp.bfloat16),
+            pltpu.VMEM((rows, chunk), jnp.bfloat16),
+        ],
+        compiler_params=parallel,
+        name="spread",
+    )(first, basis_arr, own)
+
+    def exchange(value):
+        value = value.reshape(devices, share, rows)
+        value = lax.all_to_all(value, MESH_AXES, split_axis=0, concat_axis=0, tiled=True)
+        return value.reshape(NG, rows)
+
+    received = exchange(charge)
+    at = ((pen_at * groups + grp_at) * domains + dom_at) * share + lax.iota(jnp.int32, share)
+    own_line = jnp.asarray(line.astype(np.float32))[at]
+    own_sq = jnp.asarray((freq * freq).astype(np.float32))[at]
+    returned = pl.pallas_call(
+        lambda *refs: spectral_kernel(*refs, sizes=sizes),
+        in_specs=[smem_spec(), smem_spec()] + [whole_spec((NG, NG))] * 5 + [whole_spec((NG, rows))],
+        out_specs=whole_spec((NG, rows)),
+        out_shape=jax.ShapeDtypeStruct((NG, rows), jnp.float32),
+        scratch_shapes=[
+            pltpu.VMEM((pencils * block, rows), jnp.float32),
+            pltpu.VMEM((slab * block, NG), jnp.float32),
+        ],
+        grid=(),
+        name="spectral",
+    )(own_line, own_sq, basis_arr, jnp.asarray(mixed), jnp.asarray(mixed.T), plane, plane_sq, received)
+    coefs = exchange(returned)
+
+    nearby = neighbours(own, domains, pencils)
+    steps = np.arange(9)
+    dom_seen = dom_at + jnp.asarray(steps // 3 - 1)
+    pen_seen = pen_at + jnp.asarray(steps % 3 - 1)
+    wrap = jnp.stack([dom_seen // domains, pen_seen // pencils]).astype(jnp.float32)
+    short_out = pl.pallas_call(
+        lambda *refs: pair_kernel(
+            *refs,
+            factors=(2.0 * domains, 2.0 * pencils, 2.0 * domains),
+            scale=2.0 / math.sqrt(atom_count / domains),
+        ),
+        in_specs=[smem_spec(), smem_spec(), smem_spec(), whole_spec(nearby.shape)],
+        out_specs=whole_spec((3, atom_count)),
+        out_shape=jax.ShapeDtypeStruct((3, atom_count), jnp.float32),
+        grid=(),
+        name="pairs",
+    )(pair_home.reshape(-1), pair_other.reshape(-1), wrap, nearby)
+
+    chunk = 256
+    long_scale = -0.4 * NG / math.sqrt(NG * atom_count * devices)
+    long_out = pl.pallas_call(
+        lambda *refs: interpolate_kernel(*refs, sizes=sizes, scale=long_scale),
+        grid=(atom_count // chunk,),
+        in_specs=[
+            smem_spec(),
+            whole_spec((NG, NG)),
+            whole_spec((NG, rows)),
+            pl.BlockSpec((4, chunk), lambda i: (0, i)),
+        ],
+        out_specs=pl.BlockSpec((3, chunk), lambda i: (0, i)),
+        out_shape=jax.ShapeDtypeStruct((3, atom_count), jnp.float32),
+        scratch_shapes=[
+            pltpu.VMEM((rows, 3 * NG), jnp.bfloat16),
+            pltpu.VMEM((rows, 2 * chunk), jnp.float32),
+        ],
+        compiler_params=parallel,
+        name="interpolate",
+    )(first, basis_arr, coefs, own)
+    return (short_out.reshape(3, 1, 1, atom_count), long_out.reshape(3, 1, 1, atom_count))
+
+
 def solution(mesh):
     placed = (P(None, "grp", "dom", "pen"), P("grp", "dom", "pen"), P("grp", "dom", "pen"))
+
+    def body(atoms, pair_home, pair_other):
+        sizes = fast_sizes(
+            mesh.shape["grp"], mesh.shape["dom"], mesh.shape["pen"], atoms.shape[3]
+        )
+        if sizes is None:
+            return on_device(atoms, pair_home, pair_other)
+        return fast_on_device(atoms, pair_home, pair_other, sizes=sizes)
+
     return jax.shard_map(
-        on_device,
+        body,
         mesh=mesh,
         in_specs=placed,
         out_specs=(P(None, "grp", "dom", "pen"), P(None, "grp", "dom", "pen")),

time: 636 us -> 103 us (0.16); the launches traced: 624 us -> 102 us
  matrix products: 189 us -> 0 us
  local copies, waits for them, and re-layouts: 147 us -> 15 us
  other arithmetic: 125 us -> 1.24 us
  Pallas kernels: 0 us -> 53.3 us
  blocking collectives: 51.7 us -> 0 us
  waiting for transfers between devices: 53.7 us -> 11 us
  starting transfers between devices: 40.4 us -> 21 us
  between operations: 15.3 us -> 0.79 us
    dot_general x69 -> x0, matrix products: 189 us -> none  [the longest x52 100 us: matmul(): jnp.dot(left, right, precision=exact_precision, preferred_element_type=jn...]
    mul x54 -> x0, local copies, waits for them, and re-layouts: 81.3 us -> none  [the longest x16 40.2 us: interpolate(): grad_z = jnp.sum(weight_y[:, None] * weight_x[None] * slope_z, axis=(0, 1))]
    mul x120 -> x0, other arithmetic: 78.5 us -> none  [the longest x16 39.5 us: spread_step(): paired = weight_x[:, None, :] * weighted_y[None, :, :]]
    pallas_call x0 -> x4, Pallas kernels: none -> 53.3 us  [the longest x1 19.4 us: fast_on_device(): pl.pallas_call(lambda *refs: pair_kernel(*refs, factors=(2.0 * domains, 2...]
    all_gather x2 -> x0, blocking collectives: 51.7 us -> none  [the longest x1 26.2 us: on_device(): lax.all_gather(slab_real, 'grp', axis=2, tiled=True)]
    all_to_all x8 -> x2, starting transfers between devices: 32.6 us -> 6.09 us  [exchange(): lax.all_to_all(value, MESH_AXES, split_axis=0, concat_axis=0, tiled=True)]
    reduce_scatter x2 -> x0, waiting for transfers between devices: 22.1 us -> none  [the longest x1 12 us: on_device(): lax.psum_scatter(z_real, 'grp', scatter_dimension=1, tiled=True)]
    all_to_all x8 -> x0, other arithmetic: 13 us -> none  [the longest x1 2.31 us: on_device(): lax.all_to_all(fx_imag, 'pen', split_axis=0, concat_axis=1, tiled=True)]
  transfers between devices with their start and end apart: 16 -> 10, of which waited for: 12 -> 2; matrix products, arithmetic and copies ran while one was open for 11% -> 10% of each run, Pallas kernels for 0% -> 34%
where the time goes in v1:
time: 103 us; the launch traced here: 102 us
  Pallas kernels  53.3 us (52%)
  starting transfers between devices  21 us (20%)
  local copies, waits for them, and re-layouts  15 us (15%)
  waiting for transfers between devices  11 us (11%)
  other arithmetic  1.24 us (1%)
    pallas_call x1, Pallas kernels, fast_on_device(): pl.pallas_call(lambda *refs: pair_kernel(*refs, factors=(2.0 * domains, 2...  19.4 us
    pallas_call x1, Pallas kernels, fast_on_device(): pl.pallas_call(lambda *refs: interpolate_kernel(*refs, sizes=sizes, scale...  18.2 us
    ppermute x8, starting transfers between devices, neighbours(): found.append(lax.ppermute(block, ('dom', 'pen'), route))  14.9 us
    pallas_call x1, Pallas kernels, fast_on_device(): pl.pallas_call(lambda *refs: spread_kernel(*refs, sizes=sizes), grid=(ato...  10.9 us
    ppermute x8, waiting for transfers between devices, neighbours(): found.append(lax.ppermute(block, ('dom', 'pen'), route))  7.34 us
    unnamed x23, local copies, waits for them, and re-layouts  6.32 us
    all_to_all x2, starting transfers between devices, exchange(): lax.all_to_all(value, MESH_AXES, split_axis=0, concat_axis=0, tiled=True)  6.09 us
    pallas_call x1, Pallas kernels, fast_on_device(): pl.pallas_call(lambda *refs: spectral_kernel(*refs, sizes=sizes), in_spec...  4.92 us
  transfers between devices with their start and end apart: 10, of which 2 were waited for; matrix products, arithmetic and copies ran while one was open for 10% of the time, Pallas kernels for 34%

profile of v1, /device:TPU:0, one launch (start us, length us, event | category | flops | bytes accessed | tf_op | source)
XLA Modules:
  0.0 102.4 jit_solution(4008118372272192117)
XLA Ops:
  0.6 1.5 %copy.22 = f32[4,1,1,4096]{3,0,1,2:T(4,128)} copy(f32[4,1,1,4096]{3,2,1,0:T(1,128)} %param.12) | data formatting | bytes 131072
  2.1 2.5 %collective-permute-start = (f32[4,4096]{1,0:T(4,128)}, f32[4,4096]{1,0:T(4,128)S(1)}, u32[]{:S(2)}, u32[]{:S(2)}) collective-permute-start(f32[4,4096]{1,0:T(4,128)} %bitcast.32.refs_2_.refs_3_), channel_id=1, source_target_pairs={{15,0},{12,1},{13,2},{14,3},{3,4},{0,5},{1,6},{2,7},{7,8},{4,9},{5... | collective-permute-start | bytes 196616 | tf_op jit(solution)/shard_map/ppermute | solution.py:633
  4.6 1.6 %collective-permute-start.1 = (f32[4,4096]{1,0:T(4,128)}, f32[4,4096]{1,0:T(4,128)S(1)}, u32[]{:S(2)}, u32[]{:S(2)}) collective-permute-start(f32[4,4096]{1,0:T(4,128)} %bitcast.32.refs_2_.refs_3_), channel_id=1, source_target_pairs={{12,0},{13,1},{14,2},{15,3},{0,4},{1,5},{2,6},{3,7},{4,8},{5,9},{6... | collective-permute-start | bytes 196616 | tf_op jit(solution)/shard_map/ppermute | solution.py:633
  6.3 2.2 %collective-permute-start.2 = (f32[4,4096]{1,0:T(4,128)}, f32[4,4096]{1,0:T(4,128)S(1)}, u32[]{:S(2)}, u32[]{:S(2)}) collective-permute-start(f32[4,4096]{1,0:T(4,128)} %bitcast.32.refs_2_.refs_3_), channel_id=1, source_target_pairs={{13,0},{14,1},{15,2},{12,3},{1,4},{2,5},{3,6},{0,7},{5,8},{6,9},{7... | collective-permute-start | bytes 196616 | tf_op jit(solution)/shard_map/ppermute | solution.py:633
  8.5 0.0 collective-permute-start.3
  8.5 3.8 %collective-permute-start.4 = (f32[4,4096]{1,0:T(4,128)}, f32[4,4096]{1,0:T(4,128)S(1)}, u32[]{:S(2)}, u32[]{:S(2)}) collective-permute-start(f32[4,4096]{1,0:T(4,128)} %bitcast.32.refs_2_.refs_3_), channel_id=1, source_target_pairs={{1,0},{2,1},{3,2},{0,3},{5,4},{6,5},{7,6},{4,7},{9,8},{10,9},{11,1... | collective-permute-start | bytes 196616 | tf_op jit(solution)/shard_map/ppermute | solution.py:633
  12.3 0.6 pad_add_fusion.refs_0_
  12.9 10.9 %spread.1 = f32[128,1280]{1,0:T(8,128)} custom-call(s32[2]{0:T(128)} %pad_add_fusion.refs_0_, f32[128,128]{1,0:T(8,128)} %constant.63.clone.refs_1_.refs_2_, f32[4,4096]{1,0:T(4,128)} %bitcast.32.refs_2_.refs_3_), custom_call_target="tpu_custom_call" | custom-call | tf_op jit(solution)/shard_map/spread/pallas_call | solution.py:666
  23.8 2.1 %reshape.51 = f32[32,4,1280]{2,1,0:T(4,128)} reshape(f32[128,1280]{1,0:T(8,128)} %spread.1) | data formatting | bytes 1310720 | tf_op jit(solution)/shard_map/reshape | solution.py:686
  25.9 0.0 copy-start.1
  25.9 2.7 %all-to-all-start = ((f32[32,4,1280]{2,1,0:T(4,128)}), f32[32,4,1280]{2,1,0:T(4,128)S(1)}, u32[]{:S(2)}, u32[]{:S(2)}) async-start(f32[32,4,1280]{2,1,0:T(4,128)} %reshape.51), calls=%async_computation | async-start | bytes 1310720 | tf_op jit(solution)/shard_map/all_to_all | solution.py:687
  28.7 0.0 copy-done.1
  28.7 0.0 copy-start
  28.7 1.1 %gather_fusion = f32[4]{0:T(128)} fusion(f32[128]{0:T(128)S(1)} %copy-done.1, s32[1024]{0:T(1024)S(1)} %pad_clamp_fusion), kind=kCustom, calls=%fused_computation | custom fusion | bytes 48 | tf_op jit(solution)/shard_map/gather | solution.py:692
  29.9 0.0 copy-done
  29.9 0.0 copy-start.4
  29.9 0.0 copy-start.5
  29.9 1.2 %gather_fusion.1 = f32[4]{0:T(128)} fusion(f32[128]{0:T(128)S(1)} %copy-done, s32[1024]{0:T(1024)S(1)} %pad_clamp_fusion), kind=kCustom, calls=%fused_computation.1 | custom fusion | bytes 48 | tf_op jit(solution)/shard_map/gather | solution.py:693
  31.1 0.0 copy-done.4
  31.1 0.0 copy-done.5
  31.1 0.6 add_convert_fusion.refs_2_
  31.7 0.0 collective-permute-done
  31.7 2.3 %collective-permute-start.5 = (f32[4,4096]{1,0:T(4,128)}, f32[4,4096]{1,0:T(4,128)S(1)}, u32[]{:S(2)}, u32[]{:S(2)}) collective-permute-start(f32[4,4096]{1,0:T(4,128)} %bitcast.32.refs_2_.refs_3_), channel_id=1, source_target_pairs={{7,0},{4,1},{5,2},{6,3},{11,4},{8,5},{9,6},{10,7},{15,8},{12,9},{1... | collective-permute-start | bytes 196616 | tf_op jit(solution)/shard_map/ppermute | solution.py:633
  34.0 0.0 collective-permute-done.1
  34.0 0.6 collective-permute-start.6
  34.6 0.0 collective-permute-done.2
  34.7 1.8 %collective-permute-start.7 = (f32[4,4096]{1,0:T(4,128)}, f32[4,4096]{1,0:T(4,128)S(1)}, u32[]{:S(2)}, u32[]{:S(2)}) collective-permute-start(f32[4,4096]{1,0:T(4,128)} %bitcast.32.refs_2_.refs_3_), channel_id=1, source_target_pairs={{5,0},{6,1},{7,2},{4,3},{9,4},{10,5},{11,6},{8,7},{13,8},{14,9},{1... | collective-permute-start | bytes 196616 | tf_op jit(solution)/shard_map/ppermute | solution.py:633
  36.5 0.0 copy-start.3
  36.5 0.0 collective-permute-done.3
  36.5 0.8 copy-done.3
  37.3 0.1 bitcast_dynamic-update-slice_fusion
  37.4 0.0 collective-permute-done.4
  37.4 7.3 %collective-permute-done.5 = f32[4,4096]{1,0:T(4,128)S(1)} collective-permute-done((f32[4,4096]{1,0:T(4,128)}, f32[4,4096]{1,0:T(4,128)S(1)}, u32[]{:S(2)}, u32[]{:S(2)}) %collective-permute-start.5) | collective-permute-done | bytes 65568 | tf_op jit(solution)/shard_map/ppermute | solution.py:633
  44.8 3.7 %all-to-all-done = f32[32,4,1280]{2,1,0:T(4,128)S(1)} async-done(((f32[32,4,1280]{2,1,0:T(4,128)}), f32[32,4,1280]{2,1,0:T(4,128)S(1)}, u32[]{:S(2)}, u32[]{:S(2)}) %all-to-all-start) | async-done | bytes 655392 | tf_op jit(solution)/shard_map/all_to_all | solution.py:687
  48.4 1.1 %reshape.52.refs_7_ = f32[128,1280]{1,0:T(8,128)} reshape(f32[32,4,1280]{2,1,0:T(4,128)S(1)} %all-to-all-done) | data formatting | bytes 1310720 | tf_op jit(solution)/shard_map/reshape | solution.py:688
  49.5 4.9 %spectral.1 = f32[128,1280]{1,0:T(8,128)} custom-call(f32[4]{0:T(128)} %gather_fusion, f32[4]{0:T(128)} %gather_fusion.1, f32[128,128]{1,0:T(8,128)} %constant.63.clone.refs_1_.refs_2_, f32[128,128]{1,0:T(8,128)} %constant.66.clone.refs_3_, f32[128,128]{1,0:T(8,128)} %constant.67.clone.refs_4_, f32[128,128]{1,0:T(8,128)} %constant.61.clone.refs_5_, ...), custom_call_target="tpu_custom_call" | custom-call | tf_op jit(solution)/shard_map/spectral/pallas_call | solution.py:694
  54.4 2.1 %reshape.53 = f32[32,4,1280]{2,1,0:T(4,128)} reshape(f32[128,1280]{1,0:T(8,128)} %spectral.1) | data formatting | bytes 1310720 | tf_op jit(solution)/shard_map/reshape | solution.py:686
  56.5 3.3 %all-to-all-start.1 = ((f32[32,4,1280]{2,1,0:T(4,128)}), f32[32,4,1280]{2,1,0:T(4,128)S(1)}, u32[]{:S(2)}, u32[]{:S(2)}) async-start(f32[32,4,1280]{2,1,0:T(4,128)} %reshape.53), calls=%async_computation.1 | async-start | bytes 1310720 | tf_op jit(solution)/shard_map/all_to_all | solution.py:687
  59.9 0.0 collective-permute-done.6
  59.9 0.0 collective-permute-done.7
  59.9 0.0 copy-start.2
  59.9 0.8 copy-done.2
  60.8 19.4 %pairs.1 = f32[3,4096]{1,0:T(4,128)} custom-call(s32[64]{0:T(128)} %bitcast.35, s32[64]{0:T(128)} %bitcast.36, f32[2,9]{1,0:T(2,128)} %add_convert_fusion.refs_2_, f32[9,4,4096]{2,1,0:T(4,128)} %copy-done.2), custom_call_target="tpu_custom_call" | custom-call | tf_op jit(solution)/shard_map/pairs/pallas_call | solution.py:713
  80.1 1.5 %copy.16 = f32[3,1,1,4096]{3,2,1,0:T(1,128)} copy(f32[3,1,1,4096]{3,0,2,1:T(4,128)} %bitcast.34) | data formatting | bytes 98304
  81.6 0.0 all-to-all-done.1
  81.6 1.1 %reshape.54.refs_2_ = f32[128,1280]{1,0:T(8,128)} reshape(f32[32,4,1280]{2,1,0:T(4,128)S(1)} %all-to-all-done.1) | data formatting | bytes 1310720 | tf_op jit(solution)/shard_map/reshape | solution.py:688
  82.7 18.2 %interpolate.1 = f32[3,4096]{1,0:T(4,128)} custom-call(s32[2]{0:T(128)} %pad_add_fusion.refs_0_, f32[128,128]{1,0:T(8,128)} %constant.63.clone.refs_1_.refs_2_, f32[128,1280]{1,0:T(8,128)} %reshape.54.refs_2_, f32[4,4096]{1,0:T(4,128)} %bitcast.32.refs_2_.refs_3_), custom_call_target="tpu_custom_call" | custom-call | tf_op jit(solution)/shard_map/interpolate/pallas_call | solution.py:728
  100.9 1.5 %copy.17 = f32[3,1,1,4096]{3,2,1,0:T(1,128)} copy(f32[3,1,1,4096]{3,0,2,1:T(4,128)} %bitcast.33) | data formatting | bytes 98304
  (11 shorter events, 0.1 us)
Async XLA Ops:
  2.1 29.5 %collective-permute-start = (f32[4,4096]{1,0:T(4,128)}, f32[4,4096]{1,0:T(4,128)S(1)}, u32[]{:S(2)}, u32[]{:S(2)}) collective-permute-start(f32[4,4096]{1,0:T(4,128)} %bitcast.32.refs_2_.refs_3_), channel_id=1, source_target_pairs={{15,0},{12,1},{13,2},{14,3},{3,4},{0,5},{1,6},{2,7},{7,8},{4,9},{5... | collective-permute-start | bytes 196616 | tf_op jit(solution)/shard_map/ppermute | solution.py:633
  4.6 29.4 %collective-permute-start.1 = (f32[4,4096]{1,0:T(4,128)}, f32[4,4096]{1,0:T(4,128)S(1)}, u32[]{:S(2)}, u32[]{:S(2)}) collective-permute-start(f32[4,4096]{1,0:T(4,128)} %bitcast.32.refs_2_.refs_3_), channel_id=1, source_target_pairs={{12,0},{13,1},{14,2},{15,3},{0,4},{1,5},{2,6},{3,7},{4,8},{5,9},{6... | collective-permute-start | bytes 196616 | tf_op jit(solution)/shard_map/ppermute | solution.py:633
  6.3 28.4 %collective-permute-start.2 = (f32[4,4096]{1,0:T(4,128)}, f32[4,4096]{1,0:T(4,128)S(1)}, u32[]{:S(2)}, u32[]{:S(2)}) collective-permute-start(f32[4,4096]{1,0:T(4,128)} %bitcast.32.refs_2_.refs_3_), channel_id=1, source_target_pairs={{13,0},{14,1},{15,2},{12,3},{1,4},{2,5},{3,6},{0,7},{5,8},{6,9},{7... | collective-permute-start | bytes 196616 | tf_op jit(solution)/shard_map/ppermute | solution.py:633
  8.5 28.1 %collective-permute-start.3 = (f32[4,4096]{1,0:T(4,128)}, f32[4,4096]{1,0:T(4,128)S(1)}, u32[]{:S(2)}, u32[]{:S(2)}) collective-permute-start(f32[4,4096]{1,0:T(4,128)} %bitcast.32.refs_2_.refs_3_), channel_id=1, source_target_pairs={{3,0},{0,1},{1,2},{2,3},{7,4},{4,5},{5,6},{6,7},{11,8},{8,9},{9,10... | collective-permute-start | bytes 196616 | tf_op jit(solution)/shard_map/ppermute | solution.py:633
  8.5 28.9 %collective-permute-start.4 = (f32[4,4096]{1,0:T(4,128)}, f32[4,4096]{1,0:T(4,128)S(1)}, u32[]{:S(2)}, u32[]{:S(2)}) collective-permute-start(f32[4,4096]{1,0:T(4,128)} %bitcast.32.refs_2_.refs_3_), channel_id=1, source_target_pairs={{1,0},{2,1},{3,2},{0,3},{5,4},{6,5},{7,6},{4,7},{9,8},{10,9},{11,1... | collective-permute-start | bytes 196616 | tf_op jit(solution)/shard_map/ppermute | solution.py:633
  25.9 2.8 %copy-start.1 = (f32[128]{0:T(128)S(1)}, f32[128]{0:T(128)}, u32[]{:S(2)}) copy-start(f32[128]{0:T(128)} %constant.64.clone) | copy-start | bytes 1540
  25.9 22.5 %all-to-all-start = ((f32[32,4,1280]{2,1,0:T(4,128)}), f32[32,4,1280]{2,1,0:T(4,128)S(1)}, u32[]{:S(2)}, u32[]{:S(2)}) async-start(f32[32,4,1280]{2,1,0:T(4,128)} %reshape.51), calls=%async_computation | async-start | bytes 1310720 | tf_op jit(solution)/shard_map/all_to_all | solution.py:687
  28.7 1.2 %copy-start = (f32[128]{0:T(128)S(1)}, f32[128]{0:T(128)}, u32[]{:S(2)}) copy-start(f32[128]{0:T(128)} %constant.65.clone) | copy-start | bytes 1540
  29.9 1.2 %copy-start.4 = (s32[9]{0:T(128)S(1)}, s32[9]{0:T(128)}, u32[]{:S(2)}) copy-start(s32[9]{0:T(128)} %constant.69.clone) | copy-start | bytes 112
  29.9 1.2 %copy-start.5 = (s32[9]{0:T(128)S(1)}, s32[9]{0:T(128)}, u32[]{:S(2)}) copy-start(s32[9]{0:T(128)} %constant.68.clone) | copy-start | bytes 112
  31.7 13.1 %collective-permute-start.5 = (f32[4,4096]{1,0:T(4,128)}, f32[4,4096]{1,0:T(4,128)S(1)}, u32[]{:S(2)}, u32[]{:S(2)}) collective-permute-start(f32[4,4096]{1,0:T(4,128)} %bitcast.32.refs_2_.refs_3_), channel_id=1, source_target_pairs={{7,0},{4,1},{5,2},{6,3},{11,4},{8,5},{9,6},{10,7},{15,8},{12,9},{1... | collective-permute-start | bytes 196616 | tf_op jit(solution)/shard_map/ppermute | solution.py:633
  34.0 25.8 %collective-permute-start.6 = (f32[4,4096]{1,0:T(4,128)}, f32[4,4096]{1,0:T(4,128)S(1)}, u32[]{:S(2)}, u32[]{:S(2)}) collective-permute-start(f32[4,4096]{1,0:T(4,128)} %bitcast.32.refs_2_.refs_3_), channel_id=1, source_target_pairs={{4,0},{5,1},{6,2},{7,3},{8,4},{9,5},{10,6},{11,7},{12,8},{13,9},{1... | collective-permute-start | bytes 196616 | tf_op jit(solution)/shard_map/ppermute | solution.py:633
  34.7 25.2 %collective-permute-start.7 = (f32[4,4096]{1,0:T(4,128)}, f32[4,4096]{1,0:T(4,128)S(1)}, u32[]{:S(2)}, u32[]{:S(2)}) collective-permute-start(f32[4,4096]{1,0:T(4,128)} %bitcast.32.refs_2_.refs_3_), channel_id=1, source_target_pairs={{5,0},{6,1},{7,2},{4,3},{9,4},{10,5},{11,6},{8,7},{13,8},{14,9},{1... | collective-permute-start | bytes 196616 | tf_op jit(solution)/shard_map/ppermute | solution.py:633
  36.5 0.8 copy-start.3
  56.5 25.1 %all-to-all-start.1 = ((f32[32,4,1280]{2,1,0:T(4,128)}), f32[32,4,1280]{2,1,0:T(4,128)S(1)}, u32[]{:S(2)}, u32[]{:S(2)}) async-start(f32[32,4,1280]{2,1,0:T(4,128)} %reshape.53), calls=%async_computation.1 | async-start | bytes 1310720 | tf_op jit(solution)/shard_map/all_to_all | solution.py:687
  59.9 0.8 copy-start.2

commit v2 on v1

--- a/solution.py
+++ b/solution.py
@@ -114,9 +114,9 @@
     batches = spread_atoms.reshape(4, -1, span_size).transpose(1, 0, 2)
 
     def spread_step(totals, atom_batch):
-        weight_x, unused_x = spline_rows(atom_batch[0], first_x, slab_cells, grid_cells)
-        weight_y, unused_y = spline_rows(atom_batch[1], first_y, column, grid_cells)
-        weight_z, unused_z = spline_rows(atom_batch[2], 0, grid_cells, grid_cells)
+        weight_x, _ = spline_rows(atom_batch[0], first_x, slab_cells, grid_cells)
+        weight_y, _ = spline_rows(atom_batch[1], first_y, column, grid_cells)
+        weight_z, _ = spline_rows(atom_batch[2], 0, grid_cells, grid_cells)
         weighted_y = weight_y * atom_batch[3][None, :]
         paired = weight_x[:, None, :] * weighted_y[None, :, :]
         paired = paired.reshape(slab_cells * column, span_size)
@@ -129,7 +129,7 @@
         )
         return (totals + product, None)
 
-    totals, unused = lax.scan(
+    totals, _ = lax.scan(
         spread_step, jnp.zeros((slab_cells * column, grid_cells), jnp.float32), batches
     )
     return totals
@@ -298,7 +298,9 @@
     if NG != LANES or NG % devices or NG // domains != 32 or NG // pencils != 32:
         return None
     share = NG // devices
-    if (domains * share) % SUBLANES or atom_count % 512 or TILE != LANES:
+    if min(domains, pencils) < 4:
+        return None
+    if (domains * share) % SUBLANES or atom_count % 1024 or TILE != LANES:
         return None
     slab = NG // domains
     column = NG // pencils
@@ -376,65 +378,91 @@
     return jnp.where(place >= float(NG), place - float(NG), place)
 
 
-def spread_kernel(first_ref, basis_ref, atoms_ref, out_ref, acc_ref, high_ref, low_ref, *, sizes):
-    step = pl.program_id(0)
-    lanes = atoms_ref.shape[1]
-    rows, stride = sizes["rows"], sizes["stride"]
-    floor_x, theta_x, _ = spline_parts(atoms_ref[0:1, :])
-    floor_y, theta_y, _ = spline_parts(atoms_ref[1:2, :])
-    floor_z, theta_z, _ = spline_parts(atoms_ref[2:3, :])
-    floor_x = floor_x - first_ref[0].astype(jnp.float32)
-    floor_y = floor_y - first_ref[1].astype(jnp.float32)
-    weight_x = choose(row_ids(stride + 4, lanes) - floor_x, theta_x)
-    period = row_ids(2 * stride, lanes)
-    period = jnp.where(period >= float(stride), period - float(stride), period)
-    weight_y = choose(period - floor_y, theta_y) * atoms_ref[3:4, :]
-    weight_z = choose(z_place(floor_z, lanes), theta_z)
-    z_high, z_low = split_bf16(weight_z)
-    low_half = lax.broadcasted_iota(jnp.int32, (SUBLANES, lanes), 0) < stride % SUBLANES
-    whole = stride // SUBLANES * SUBLANES
-    for group in range(-(-rows // (4 * stride))):
-        pieces = []
-        for pair in range(2):
-            at = 4 * group + 2 * pair
-            if at >= sizes["slab"] + 4:
-                continue
-            first = jnp.broadcast_to(weight_x[at : at + 1, :], (SUBLANES, lanes))
-            second = jnp.broadcast_to(weight_x[at + 1 : at + 2, :], (SUBLANES, lanes))
-            mixed = jnp.where(low_half, first, second)
-            for tile in range(2 * stride // SUBLANES):
-                factor = first if tile < whole // SUBLANES else second
-                factor = mixed if tile == whole // SUBLANES else factor
-                pieces.append(factor * weight_y[tile * SUBLANES : (tile + 1) * SUBLANES, :])
-        start = group * 4 * stride
-        count = min(4 * stride, rows - start)
-        paired = jnp.concatenate(pieces, axis=0)[:count]
-        high, low = split_bf16(paired)
-        high_ref[start : start + count, :] = high
-        low_ref[start : start + count, :] = low
+def repeated_row(ref, table, row):
+    return ref[table, pl.ds(row, SUBLANES, stride=0), :]
+
+
+def period_ids(stride):
+    period = row_ids(2 * stride, LANES)
+    return jnp.where(period >= float(stride), period - float(stride), period)
+
+
+def spread_kernel(
+    place_ref, basis_ref, atoms_ref, out_ref, acc_ref, row_ref,
+    high_a, low_a, z_a, high_b, low_b, z_b, *, sizes
+):
+    chunk_tiles = z_a.shape[1] // LANES
+    chunks = atoms_ref.shape[1] // chunk_tiles
+    rows, stride, share = sizes["rows"], sizes["stride"], sizes["share"]
+    low_half = lax.broadcasted_iota(jnp.int32, (SUBLANES, LANES), 0) < stride % SUBLANES
+    middle = stride // SUBLANES
     contract = (((1,), (1,)), ((), ()))
-    both = jnp.concatenate([z_high, z_low], axis=0)
-    main = lax.dot_general(high_ref[...], both, contract, preferred_element_type=jnp.float32)
-    rest = lax.dot_general(low_ref[...], z_high, contract, preferred_element_type=jnp.float32)
-    total = main[:, :NG] + main[:, NG:] + rest
-
-    @pl.when(step == 0)
-    def _():
-        acc_ref[...] = total
-
-    @pl.when(step > 0)
-    def _():
-        acc_ref[...] += total
-
-    @pl.when(step == pl.num_programs(0) - 1)
-    def _():
-        out_ref[...] = lax.dot_general(
-            basis_ref[...],
-            acc_ref[...],
-            contract,
-            precision=exact_precision,
-            preferred_element_type=jnp.float32,
+
+    def build(chunk, side, high_ref, low_ref, z_ref):
+        for block in range(chunk_tiles):
+            tile = chunk * chunk_tiles + block
+            span = slice(block * LANES, (block + 1) * LANES)
+            parts = [atoms_ref[part, pl.ds(tile, 1), :] for part in range(4)]
+            floor_x, theta_x, _ = spline_parts(parts[0])
+            floor_y, theta_y, _ = spline_parts(parts[1])
+            floor_z, theta_z, _ = spline_parts(parts[2])
+            floor_x = floor_x - place_ref[0].astype(jnp.float32)
+            floor_y = floor_y - place_ref[1].astype(jnp.float32)
+            z_high, z_low = split_bf16(choose(z_place(floor_z, LANES), theta_z))
+            z_ref[:NG, span] = z_high
+            z_ref[NG:, span] = z_low
+            table = side * chunk_tiles + block
+            row_ref[table, :, :] = choose(row_ids(stride + 4, LANES) - floor_x, theta_x)
+            weight_y = choose(period_ids(stride) - floor_y, theta_y) * parts[3]
+            for group in range(-(-rows // (4 * stride))):
+                pieces = []
+                for at in range(4 * group, min(4 * group + 4, sizes["slab"] + 4), 2):
+                    first = repeated_row(row_ref, table, at)
+                    second = repeated_row(row_ref, table, at + 1)
+                    mixed = jnp.where(low_half, first, second)
+                    for step in range(2 * stride // SUBLANES):
+                        factor = first if step < middle else mixed if step == middle else second
+                        pieces.append(factor * weight_y[step * SUBLANES : (step + 1) * SUBLANES, :])
+                start = group * 4 * stride
+                count = min(4 * stride, rows - start)
+                high, low = split_bf16(jnp.concatenate(pieces[: count // SUBLANES], axis=0))
+                high_ref[start : start + count, span] = high
+                low_ref[start : start + count, span] = low
+
+    def add(high_ref, low_ref, z_ref):
+        main = lax.dot_general(
+            high_ref[...], z_ref[...], contract, preferred_element_type=jnp.float32
         )
+        rest = lax.dot_general(
+            low_ref[...], z_ref[:NG, :], contract, preferred_element_type=jnp.float32
+        )
+        acc_ref[:, : 2 * NG] += main
+        acc_ref[:, 2 * NG :] += rest
+
+    acc_ref[...] = jnp.zeros_like(acc_ref)
+    set_a, set_b = (high_a, low_a, z_a), (high_b, low_b, z_b)
+    build(0, 0, *set_a)
+
+    def two_chunks(step, carry):
+        build(2 * step + 1, 1, *set_b)
+        add(*set_a)
+        build(2 * step + 2, 0, *set_a)
+        add(*set_b)
+        return carry
+
+    lax.fori_loop(0, chunks // 2 - 1, two_chunks, 0)
+    build(chunks - 1, 1, *set_b)
+    add(*set_a)
+    add(*set_b)
+    result = lax.dot_general(
+        basis_ref[...],
+        acc_ref[:, :NG] + acc_ref[:, NG : 2 * NG] + acc_ref[:, 2 * NG :],
+        contract,
+        precision=exact_precision,
+        preferred_element_type=jnp.float32,
+    )
+    for target in range(NG // share):
+        out_ref[target, :, :] = result[target * share : (target + 1) * share, :]
 
 
 def ring_mask(lane, start, length):
@@ -445,18 +473,21 @@
 
 
 def spectral_kernel(
-    line_ref, square_ref, basis_ref, mixed_ref, mixed_t_ref, plane_ref, plane_sq_ref,
+    place_ref, line_ref, basis_ref, mixed_ref, mixed_t_ref, plane_ref, plane_sq_ref,
     in_ref, out_ref, sum_ref, work_ref, *, sizes
 ):
     block, share, stride = sizes["block"], sizes["share"], sizes["stride"]
     slab, column, groups = sizes["slab"], sizes["column"], sizes["groups"]
     pencils, rows = sizes["pencils"], sizes["rows"]
+    domains = sizes["domains"]
     for pen in range(pencils):
-        total = in_ref[pen * groups * block : (pen * groups + 1) * block, :]
-        for grp in range(1, groups):
-            start = (pen * groups + grp) * block
-            total = total + in_ref[start : start + block, :]
-        sum_ref[pen * block : (pen + 1) * block, :] = total
+        pieces = []
+        for dom in range(domains):
+            total = in_ref[pen * groups * domains + dom, :, :]
+            for grp in range(1, groups):
+                total = total + in_ref[(pen * groups + grp) * domains + dom, :, :]
+            pieces.append(total)
+        sum_ref[pen * block : (pen + 1) * block, :] = jnp.concatenate(pieces, axis=0)
     lane = lax.broadcasted_iota(jnp.int32, (block, LANES), 1)
     width = column + 3
 
@@ -493,8 +524,10 @@
     for kz in range(share):
         picked = work_ref[pl.ds(kz, NG, stride=share), :]
         spectrum = dot(mixed_ref[...], picked)
-        square = plane_sq_ref[...] + square_ref[kz]
-        factor = plane_ref[...] * line_ref[kz] / jnp.maximum(square, 1.0)
+        at = place_ref[2] + kz
+        freq = jnp.where(at > NG // 2, at - NG // 2, at)
+        square = plane_sq_ref[...] + (freq * freq).astype(jnp.float32)
+        factor = plane_ref[...] * line_ref[freq] / jnp.maximum(square, 1.0)
         factor = jnp.where(square > 0.5, factor, 0.0)
         work_ref[pl.ds(kz, NG, stride=share), :] = dot(mixed_t_ref[...], spectrum * factor)
     work_ref[...] = dot(work_ref[...], basis_ref[...])
@@ -516,126 +549,170 @@
                 value = pltpu.roll(value, shift, 1) if shift else value
                 mask = ring_mask(lane, low - tile * LANES, high - low)
                 total = jnp.where(mask, value, total)
-            for grp in range(groups):
-                start = (pen * groups + grp) * block
-                out_ref[start : start + block, tile * LANES : (tile + 1) * LANES] = total
+            span = slice(tile * LANES, (tile + 1) * LANES)
+            for dom in range(domains):
+                part = total[dom * share : (dom + 1) * share, :]
+                for grp in range(groups):
+                    out_ref[(pen * groups + grp) * domains + dom, :, span] = part
 
 
 def interpolate_kernel(
-    first_ref, basis_ref, coef_ref, atoms_ref, out_ref, pot_ref, along_ref, *, sizes, scale
+    place_ref, basis_ref, coef_ref, atoms_ref, out_ref, pot_ref, table_ref,
+    along_a, weight_a, along_b, weight_b, *, sizes, scale
 ):
-    lanes = atoms_ref.shape[1]
+    lanes = along_a.shape[1] // 2
+    tiles = lanes // LANES
+    chunks = atoms_ref.shape[1] // tiles
     rows, stride = sizes["rows"], sizes["stride"]
-
-    @pl.when(pl.program_id(0) == 0)
-    def _():
-        potential = lax.dot_general(
-            coef_ref[...],
-            basis_ref[...],
-            (((0,), (0,)), ((), ())),
-            precision=exact_precision,
-            preferred_element_type=jnp.float32,
+    coefs = jnp.concatenate([coef_ref[source, :, :] for source in range(coef_ref.shape[0])], axis=0)
+    high, low = split_bf16(coefs)
+    basis_high, basis_low = split_bf16(basis_ref[...])
+    potential = lax.dot_general(
+        jnp.concatenate([high, low, high], axis=0),
+        jnp.concatenate([basis_high, basis_high, basis_low], axis=0),
+        (((0,), (0,)), ((), ())),
+        preferred_element_type=jnp.float32,
+    )
+    high, low = split_bf16(potential)
+    pot_ref[:, :NG] = high
+    pot_ref[:, NG : 2 * NG] = low
+    pot_ref[:, 2 * NG :] = high
+    low_half = lax.broadcasted_iota(jnp.int32, (SUBLANES, LANES), 0) < stride % SUBLANES
+    middle = stride // SUBLANES
+
+    def contract_z(chunk, along_ref, weight_ref):
+        for block in range(tiles):
+            tile = chunk * tiles + block
+            floor_z, theta_z, slope_z = spline_parts(atoms_ref[2, pl.ds(tile, 1), :])
+            place = z_place(floor_z, LANES)
+            for kind, options in enumerate((theta_z, slope_z)):
+                span = slice(kind * lanes + block * LANES, kind * lanes + (block + 1) * LANES)
+                high, low = split_bf16(choose(place, options))
+                weight_ref[:NG, span] = high
+                weight_ref[NG : 2 * NG, span] = high
+                weight_ref[2 * NG :, span] = low
+        along_ref[...] = jnp.dot(
+            pot_ref[...], weight_ref[...], preferred_element_type=jnp.float32
         )
-        high, low = split_bf16(potential)
-        pot_ref[:, :NG] = high
-        pot_ref[:, NG : 2 * NG] = low
-        pot_ref[:, 2 * NG :] = high
-
-    floor_x, theta_x, slope_x = spline_parts(atoms_ref[0:1, :])
-    floor_y, theta_y, slope_y = spline_parts(atoms_ref[1:2, :])
-    floor_z, theta_z, slope_z = spline_parts(atoms_ref[2:3, :])
-    floor_x = floor_x - first_ref[0].astype(jnp.float32)
-    floor_y = floor_y - first_ref[1].astype(jnp.float32)
-    place = z_place(floor_z, lanes)
-    columns = []
-    for options in (theta_z, slope_z):
-        high, low = split_bf16(choose(place, options))
-        columns.append(jnp.concatenate([high, high, low], axis=0))
-    along_ref[...] = jnp.dot(
-        pot_ref[...], jnp.concatenate(columns, axis=1), preferred_element_type=jnp.float32
-    )
-    place = row_ids(stride + 4, lanes) - floor_x
-    weight_x, deriv_x = choose(place, theta_x), choose(place, slope_x)
-    period = row_ids(2 * stride, lanes)
-    period = jnp.where(period >= float(stride), period - float(stride), period)
-    place = period - floor_y
-    weight_y, deriv_y = choose(place, theta_y), choose(place, slope_y)
-    low_half = lax.broadcasted_iota(jnp.int32, (SUBLANES, lanes), 0) < stride % SUBLANES
-    middle = stride // SUBLANES
-    grads = [jnp.zeros((SUBLANES, lanes), jnp.float32) for axis in range(3)]
-    for at in range(0, sizes["slab"] + 3, 2):
-        sums = [[None] * 3 for axis in range(3)]
-        for tile in range(2 * stride // SUBLANES):
-            row = at * stride + tile * SUBLANES
-            if row >= rows:
-                continue
-            span = slice(tile * SUBLANES, (tile + 1) * SUBLANES)
-            along = along_ref[row : row + SUBLANES, :lanes]
-            slope = along_ref[row : row + SUBLANES, lanes:]
-            kind = 0 if tile < middle else 1 if tile == middle else 2
-            terms = (along * weight_y[span, :], along * deriv_y[span, :], slope * weight_y[span, :])
+
+    def finish(chunk, side, along_ref):
+        for block in range(tiles):
+            tile = chunk * tiles + block
+            parts = [atoms_ref[part, pl.ds(tile, 1), :] for part in (0, 1, 3)]
+            floor_x, theta_x, slope_x = spline_parts(parts[0])
+            floor_y, theta_y, slope_y = spline_parts(parts[1])
+            floor_x = floor_x - place_ref[0].astype(jnp.float32)
+            floor_y = floor_y - place_ref[1].astype(jnp.float32)
+            place = row_ids(stride + 4, LANES) - floor_x
+            kept = 2 * (side * tiles + block)
+            table_ref[kept, :, :] = choose(place, theta_x)
+            table_ref[kept + 1, :, :] = choose(place, slope_x)
+            place = period_ids(stride) - floor_y
+            weight_y, deriv_y = choose(place, theta_y), choose(place, slope_y)
+            grads = [jnp.zeros((SUBLANES, LANES), jnp.float32) for _ in range(3)]
+            for at in range(0, sizes["slab"] + 3, 2):
+                sums = [[None] * 3 for _ in range(3)]
+                for step in range(2 * stride // SUBLANES):
+                    row = at * stride + step * SUBLANES
+                    if row >= rows:
+                        continue
+                    here = slice(row, row + SUBLANES)
+                    span = slice(step * SUBLANES, (step + 1) * SUBLANES)
+                    along = along_ref[here, block * LANES : (block + 1) * LANES]
+                    slope = along_ref[here, lanes + block * LANES : lanes + (block + 1) * LANES]
+                    kind = 0 if step < middle else 1 if step == middle else 2
+                    terms = (along * weight_y[span], along * deriv_y[span], slope * weight_y[span])
+                    for axis in range(3):
+                        held = sums[axis][kind]
+                        sums[axis][kind] = terms[axis] if held is None else held + terms[axis]
+                factors = []
+                for table in range(2):
+                    first = repeated_row(table_ref, kept + table, at)
+                    second = repeated_row(table_ref, kept + table, at + 1)
+                    factors.append((first, jnp.where(low_half, first, second), second))
+                for axis, table in enumerate((1, 0, 0)):
+                    for kind in range(3):
+                        grads[axis] = grads[axis] + sums[axis][kind] * factors[table][kind]
+            charge = parts[2] * scale
             for axis in range(3):
-                held = sums[axis][kind]
-                sums[axis][kind] = terms[axis] if held is None else held + terms[axis]
-        for axis, table in enumerate((deriv_x, weight_x, weight_x)):
-            first = jnp.broadcast_to(table[at : at + 1, :], (SUBLANES, lanes))
-            second = jnp.broadcast_to(table[at + 1 : at + 2, :], (SUBLANES, lanes))
-            factors = (first, jnp.where(low_half, first, second), second)
-            for kind in range(3):
-                grads[axis] = grads[axis] + sums[axis][kind] * factors[kind]
-    charge = atoms_ref[3:4, :] * scale
-    for axis in range(3):
-        out_ref[axis : axis + 1, :] = jnp.sum(grads[axis], axis=0, keepdims=True) * charge
-
-
-def pair_kernel(home_ref, other_ref, wrap_ref, near_ref, out_ref, *, factors, scale):
-    tiles = near_ref.shape[2] // TILE
+                row = jnp.sum(grads[axis], axis=0, keepdims=True) * charge
+                out_ref[axis, pl.ds(tile, 1), :] = row
+
+    set_a, set_b = (along_a, weight_a), (along_b, weight_b)
+    contract_z(0, *set_a)
+
+    def two_chunks(step, carry):
+        contract_z(2 * step + 1, *set_b)
+        finish(2 * step, 0, along_a)
+        contract_z(2 * step + 2, *set_a)
+        finish(2 * step + 1, 1, along_b)
+        return carry
+
+    lax.fori_loop(0, chunks // 2 - 1, two_chunks, 0)
+    contract_z(chunks - 1, *set_b)
+    finish(chunks - 2, 0, along_a)
+    finish(chunks - 1, 1, along_b)
+
+
+def pair_kernel(
+    home_ref, other_ref, place_ref, near_ref, out_ref, *, factors, scale, domains, pencils, together
+):
+    tiles = near_ref.shape[2]
     out_ref[...] = jnp.zeros_like(out_ref)
-    centre = near_ref.shape[0] // 2
-
-    def one_pair(n, carry):
+
+    def wrapped(seen, count):
+        return jnp.where(seen < 0, -1.0, jnp.where(seen >= count, 1.0, 0.0))
+
+    def one_pair(n):
         home = home_ref[n]
         other = other_ref[n]
         around = other // tiles
-        home_at = pl.ds(pl.multiple_of(home * TILE, TILE), TILE)
-        other_at = pl.ds(pl.multiple_of((other - around * tiles) * TILE, TILE), TILE)
-        mine = near_ref[centre, :, home_at]
-        theirs = near_ref[around, :, other_at]
-        turned = jnp.concatenate([theirs, theirs], axis=0).T
-        delta_x = (mine[0:1, :] - wrap_ref[0, around]) - turned[:, 0:1]
-        delta_y = (mine[1:2, :] - wrap_ref[1, around]) - turned[:, 1:2]
-        delta_z = mine[2:3, :] - turned[:, 2:3]
+        tile = other - around * tiles
+        step_dom = around // 3
+        wrap_x = wrapped(place_ref[3] + step_dom - 1, domains)
+        wrap_y = wrapped(place_ref[4] + around - 3 * step_dom - 1, pencils)
+        mine = [near_ref[4, part, pl.ds(home, 1), :] for part in range(4)]
+        theirs = jnp.concatenate(
+            [near_ref[around, part, pl.ds(tile, 1), :] for part in range(4)] * 2, axis=0
+        ).T
+        delta_x = (mine[0] - wrap_x) - theirs[:, 0:1]
+        delta_y = (mine[1] - wrap_y) - theirs[:, 1:2]
+        delta_z = mine[2] - theirs[:, 2:3]
         delta_z = delta_z - jnp.floor(delta_z + 0.5)
         scaled = (delta_x * factors[0], delta_y * factors[1], delta_z * factors[2])
         square = scaled[0] * scaled[0] + scaled[1] * scaled[1] + scaled[2] * scaled[2]
-        weight = jnp.exp(-0.5 * square) * turned[:, 3:4]
-        charge = mine[3:4, :] * scale
-        for axis in range(3):
-            push = jnp.sum(scaled[axis] * weight, axis=0, keepdims=True) * charge
-            out_ref[axis : axis + 1, home_at] += push
+        weight = jnp.exp(-0.5 * square) * theirs[:, 3:4]
+        charge = mine[3] * scale
+        return home, [jnp.sum(part * weight, axis=0, keepdims=True) * charge for part in scaled]
+
+    def some_pairs(step, carry):
+        found = [one_pair(step * together + n) for n in range(together)]
+        for home, pushes in found:
+            for axis in range(3):
+                out_ref[axis, pl.ds(home, 1), :] += pushes[axis]
         return carry
 
-    lax.fori_loop(0, home_ref.shape[0], one_pair, 0)
-
-
-def neighbours(block, domains, pencils):
-    found = []
-    for step_dom in (-1, 0, 1):
-        for step_pen in (-1, 0, 1):
-            if step_dom == 0 and step_pen == 0:
-                found.append(block)
-                continue
-            route = [
-                ((dom + step_dom) % domains * pencils + (pen + step_pen) % pencils, dom * pencils + pen)
-                for dom in range(domains)
-                for pen in range(pencils)
-            ]
-            found.append(lax.ppermute(block, ("dom", "pen"), route))
-    return jnp.stack(found)
-
-
-def whole_spec(shape):
-    return pl.BlockSpec(shape, lambda *unused: (0,) * len(shape))
+    lax.fori_loop(0, home_ref.shape[0] // together, some_pairs, 0)
+
+
+def neighbours(block):
+    near = block[None]
+    for axis in ("pen", "dom"):
+        count = lax.axis_size(axis)
+        up = [(i, (i + 1) % count) for i in range(count)]
+        down = [(i, (i - 1) % count) for i in range(count)]
+        lower = lax.ppermute(near, axis, up)
+        upper = lax.ppermute(near, axis, down)
+        near = jnp.concatenate([lower, near, upper], axis=0)
+    return near
+
+
+def in_vmem(value):
+    return pltpu.with_memory_space_constraint(jnp.asarray(value), pltpu.VMEM)
+
+
+def whole_spec():
+    return pl.BlockSpec(memory_space=pltpu.VMEM)
 
 
 def smem_spec():
@@ -648,101 +725,111 @@
     slab, column, stride = sizes["slab"], sizes["column"], sizes["stride"]
     devices = groups * domains * pencils
     atom_count = atoms.shape[3]
-    own = atoms.reshape(4, atom_count)
+    tiles = atom_count // LANES
+    own = atoms.reshape(4, tiles, LANES)
     dom_at = lax.axis_index("dom")
     pen_at = lax.axis_index("pen")
     grp_at = lax.axis_index("grp")
-    first = jnp.stack([dom_at * slab, pen_at * column]).astype(jnp.int32)
+    line_at = ((pen_at * groups + grp_at) * domains + dom_at) * share
+    place = jnp.stack([dom_at * slab, pen_at * column, line_at, dom_at, pen_at]).astype(jnp.int32)
     freq, basis = real_basis()
     order = (np.arange(domains)[None, :] * slab + np.arange(slab)[:, None]).reshape(-1)
     mixed = np.ascontiguousarray(basis[:, order])
     line = line_factor(freq)
-    plane = jnp.asarray((line[:, None] * line[None, :] / np.pi).astype(np.float32))
-    plane_sq = jnp.asarray((freq[:, None] ** 2 + freq[None, :] ** 2).astype(np.float32))
+    plane = in_vmem((line[:, None] * line[None, :] / np.pi).astype(np.float32))
+    plane_sq = in_vmem((freq[:, None] ** 2 + freq[None, :] ** 2).astype(np.float32))
     basis_arr = jnp.asarray(basis)
+    message = pltpu.VMEM((devices, share, rows), jnp.float32)
+
+    nearby = in_vmem(neighbours(own))
 
     chunk = 512
-    parallel = pltpu.CompilerParams(dimension_semantics=("arbitrary",))
     charge = pl.pallas_call(
         lambda *refs: spread_kernel(*refs, sizes=sizes),
-        grid=(atom_count // chunk,),
-        in_specs=[
-            smem_spec(),
-            whole_spec((NG, NG)),
-            pl.BlockSpec((4, chunk), lambda i: (0, i)),
-        ],
-        out_specs=whole_spec((NG, rows)),
-        out_shape=jax.ShapeDtypeStruct((NG, rows), jnp.float32),
+        in_specs=[smem_spec(), whole_spec(), whole_spec()],
+        out_specs=whole_spec(),
+        out_shape=message,
         scratch_shapes=[
-            pltpu.VMEM((rows, NG), jnp.float32),
+            pltpu.VMEM((rows, 3 * NG), jnp.float32),
+            pltpu.VMEM((2 * chunk // LANES, stride + 4, LANES), jnp.float32),
+        ]
+        + [
             pltpu.VMEM((rows, chunk), jnp.bfloat16),
             pltpu.VMEM((rows, chunk), jnp.bfloat16),
-        ],
-        compiler_params=parallel,
+            pltpu.VMEM((2 * NG, chunk), jnp.bfloat16),
+        ]
+        * 2,
+        grid=(),
         name="spread",
-    )(first, basis_arr, own)
+    )(place, basis_arr, own)
 
     def exchange(value):
-        value = value.reshape(devices, share, rows)
         value = lax.all_to_all(value, MESH_AXES, split_axis=0, concat_axis=0, tiled=True)
-        return value.reshape(NG, rows)
+        return in_vmem(value)
 
     received = exchange(charge)
-    at = ((pen_at * groups + grp_at) * domains + dom_at) * share + lax.iota(jnp.int32, share)
-    own_line = jnp.asarray(line.astype(np.float32))[at]
-    own_sq = jnp.asarray((freq * freq).astype(np.float32))[at]
     returned = pl.pallas_call(
         lambda *refs: spectral_kernel(*refs, sizes=sizes),
-        in_specs=[smem_spec(), smem_spec()] + [whole_spec((NG, NG))] * 5 + [whole_spec((NG, rows))],
-        out_specs=whole_spec((NG, rows)),
-        out_shape=jax.ShapeDtypeStruct((NG, rows), jnp.float32),
+        in_specs=[smem_spec(), smem_spec()]
+        + [whole_spec()] * 5
+        + [whole_spec()],
+        out_specs=whole_spec(),
+        out_shape=message,
         scratch_shapes=[
             pltpu.VMEM((pencils * block, rows), jnp.float32),
             pltpu.VMEM((slab * block, NG), jnp.float32),
         ],
         grid=(),
         name="spectral",
-    )(own_line, own_sq, basis_arr, jnp.asarray(mixed), jnp.asarray(mixed.T), plane, plane_sq, received)
+    )(
+        place,
+        jnp.asarray(line[: NG // 2 + 1].astype(np.float32)),
+        basis_arr,
+        in_vmem(mixed),
+        in_vmem(mixed.T),
+        plane,
+        plane_sq,
+        received,
+    )
     coefs = exchange(returned)
 
-    nearby = neighbours(own, domains, pencils)
-    steps = np.arange(9)
-    dom_seen = dom_at + jnp.asarray(steps // 3 - 1)
-    pen_seen = pen_at + jnp.asarray(steps % 3 - 1)
-    wrap = jnp.stack([dom_seen // domains, pen_seen // pencils]).astype(jnp.float32)
+    out_shape = jax.ShapeDtypeStruct((3, tiles, LANES), jnp.float32)
+    pairs = pair_home.size
     short_out = pl.pallas_call(
         lambda *refs: pair_kernel(
             *refs,
             factors=(2.0 * domains, 2.0 * pencils, 2.0 * domains),
             scale=2.0 / math.sqrt(atom_count / domains),
+            domains=domains,
+            pencils=pencils,
+            together=math.gcd(4, pairs),
         ),
-        in_specs=[smem_spec(), smem_spec(), smem_spec(), whole_spec(nearby.shape)],
-        out_specs=whole_spec((3, atom_count)),
-        out_shape=jax.ShapeDtypeStruct((3, atom_count), jnp.float32),
+        in_specs=[smem_spec(), smem_spec(), smem_spec(), whole_spec()],
+        out_specs=whole_spec(),
+        out_shape=out_shape,
         grid=(),
         name="pairs",
-    )(pair_home.reshape(-1), pair_other.reshape(-1), wrap, nearby)
+    )(pair_home.reshape(-1), pair_other.reshape(-1), place, nearby)
 
     chunk = 256
     long_scale = -0.4 * NG / math.sqrt(NG * atom_count * devices)
     long_out = pl.pallas_call(
         lambda *refs: interpolate_kernel(*refs, sizes=sizes, scale=long_scale),
-        grid=(atom_count // chunk,),
-        in_specs=[
-            smem_spec(),
-            whole_spec((NG, NG)),
-            whole_spec((NG, rows)),
-            pl.BlockSpec((4, chunk), lambda i: (0, i)),
-        ],
-        out_specs=pl.BlockSpec((3, chunk), lambda i: (0, i)),
-        out_shape=jax.ShapeDtypeStruct((3, atom_count), jnp.float32),
+        in_specs=[smem_spec(), whole_spec(), whole_spec(), whole_spec()],
+        out_specs=whole_spec(),
+        out_shape=out_shape,
         scratch_shapes=[
             pltpu.VMEM((rows, 3 * NG), jnp.bfloat16),
+            pltpu.VMEM((4 * chunk // LANES, stride + 4, LANES), jnp.float32),
+        ]
+        + [
             pltpu.VMEM((rows, 2 * chunk), jnp.float32),
-        ],
-        compiler_params=parallel,
+            pltpu.VMEM((3 * NG, 2 * chunk), jnp.bfloat16),
+        ]
+        * 2,
+        grid=(),
         name="interpolate",
-    )(first, basis_arr, coefs, own)
+    )(place, basis_arr, coefs, own)
     return (short_out.reshape(3, 1, 1, atom_count), long_out.reshape(3, 1, 1, atom_count))
 
 

time: 103 us -> 97.6 us (0.948)
  blocking collectives: 0 us -> 25.1 us
  local copies, waits for them, and re-layouts: 15 us -> 0.75 us
  starting transfers between devices: 21 us -> 8.88 us
  Pallas kernels: 53.3 us -> 41.9 us
  waiting for transfers between devices: 11 us -> 18.8 us
  other arithmetic: 1.24 us -> 0.01 us
    all_to_all x0 -> x1, blocking collectives: none -> 25.1 us  [exchange(): lax.all_to_all(value, MESH_AXES, split_axis=0, concat_axis=0, tiled=True)]
    ppermute x8 -> x4, waiting for transfers between devices: 7.34 us -> 18.8 us  [the longest x2 10.1 us: neighbours(): upper = lax.ppermute(near, axis, down)]
    ppermute x8 -> x4, starting transfers between devices: 14.9 us -> 5.47 us  [the longest x2 5.41 us: neighbours(): upper = lax.ppermute(near, axis, down)]
    pallas_call x1, Pallas kernels: 19.4 us -> 10.2 us  [fast_on_device(): pl.pallas_call(lambda *refs: pair_kernel(*refs, factors=(2.0 * domains, 2...]
    reshape x4 -> x0, local copies, waits for them, and re-layouts: 6.35 us -> none  [the longest x2 4.22 us: exchange(): value = value.reshape(devices, share, rows)]
    unnamed x23 -> x14, local copies, waits for them, and re-layouts: 6.32 us -> 0.07 us
    all_to_all x2 -> x1, waiting for transfers between devices: 3.66 us -> 0.01 us  [exchange(): lax.all_to_all(value, MESH_AXES, split_axis=0, concat_axis=0, tiled=True)]
    all_to_all x2 -> x1, starting transfers between devices: 6.09 us -> 3.41 us  [exchange(): lax.all_to_all(value, MESH_AXES, split_axis=0, concat_axis=0, tiled=True)]
  transfers between devices with their start and end apart: 10 -> 5, of which waited for: 2 -> 4; matrix products, arithmetic and copies ran while one was open for 10% -> 0% of each run, Pallas kernels for 34% -> 11%
where the time goes in v2:
time: 97.6 us; the launch traced here: 96.2 us
  Pallas kernels  41.9 us (43%)
  blocking collectives  25.1 us (26%)
  waiting for transfers between devices  18.8 us (19%)
  starting transfers between devices  8.88 us (9%)
    all_to_all x1, blocking collectives, exchange(): lax.all_to_all(value, MESH_AXES, split_axis=0, concat_axis=0, tiled=True)  25.1 us
    pallas_call x1, Pallas kernels, fast_on_device(): pl.pallas_call(lambda *refs: interpolate_kernel(*refs, sizes=sizes, scale...  16.3 us
    pallas_call x1, Pallas kernels, fast_on_device(): pl.pallas_call(lambda *refs: spread_kernel(*refs, sizes=sizes), in_specs=...  10.9 us
    pallas_call x1, Pallas kernels, fast_on_device(): pl.pallas_call(lambda *refs: pair_kernel(*refs, factors=(2.0 * domains, 2...  10.2 us
    ppermute x2, waiting for transfers between devices, neighbours(): upper = lax.ppermute(near, axis, down)  10.1 us
    ppermute x2, waiting for transfers between devices, neighbours(): lower = lax.ppermute(near, axis, up)  8.7 us
    ppermute x2, starting transfers between devices, neighbours(): upper = lax.ppermute(near, axis, down)  5.41 us
    pallas_call x1, Pallas kernels, fast_on_device(): pl.pallas_call(lambda *refs: spectral_kernel(*refs, sizes=sizes), in_spec...  4.5 us
  transfers between devices with their start and end apart: 5, of which 4 were waited for; matrix products, arithmetic and copies ran while one was open for 0% of the time, Pallas kernels for 11%

profile of v2, /device:TPU:0, one launch (start us, length us, event | category | flops | bytes accessed | tf_op | source)
XLA Modules:
  0.0 96.2 jit_solution(14990019457347364369)
XLA Ops:
  0.6 0.7 stack.23.refs_2_.refs_0_
  1.3 10.9 %spread.1 = f32[32,4,1280]{2,1,0:T(4,128)S(1)} custom-call(s32[5]{0:T(128)} %stack.23.refs_2_.refs_0_, f32[128,128]{1,0:T(8,128)} %constant.33.clone.refs_1_.refs_2_, f32[4,32,128]{2,1,0:T(8,128)} %bitcast.11), custom_call_target="tpu_custom_call" | custom-call | tf_op jit(solution)/shard_map/spread/pallas_call | solution.py:747
  12.2 0.0 copy-start
  12.2 0.0 copy-start.1
  12.2 0.0 copy-start.2
  12.2 0.0 copy-start.3
  12.2 25.1 %all_to_all.10.refs_7_ = f32[32,4,1280]{2,1,0:T(4,128)S(1)} all-to-all(f32[32,4,1280]{2,1,0:T(4,128)S(1)} %spread.1), channel_id=1, replica_groups=mesh['grp'=2,'dom'=4,'pen'=4] {'pen','grp','dom'}, dimensions={0} | all-to-all | bytes 1310720 | tf_op jit(solution)/shard_map/all_to_all | solution.py:767
  37.4 0.0 copy-done
  37.4 0.0 copy-done.1
  37.4 0.0 copy-done.2
  37.4 0.0 copy-done.3
  37.4 4.5 %spectral.1 = f32[32,4,1280]{2,1,0:T(4,128)} custom-call(s32[5]{0:T(128)} %stack.23.refs_2_.refs_0_, f32[65]{0:T(128)} %constant.34.clone.refs_1_, f32[128,128]{1,0:T(8,128)} %constant.33.clone.refs_1_.refs_2_, f32[128,128]{1,0:T(8,128)S(1)} %copy-done.1, f32[128,128]{1,0:T(8,128)S(1)} %copy-done, f32[128,128]{1,0:T(8,128)S(1)} %copy-done.3, ...), custom_call_target="tpu_custom_call" | custom-call | tf_op jit(solution)/shard_map/spectral/pallas_call | solution.py:771
  41.9 0.0 copy-start.4
  41.9 3.4 %all-to-all-start.1 = ((f32[32,4,1280]{2,1,0:T(4,128)}), f32[32,4,1280]{2,1,0:T(4,128)S(1)}, u32[]{:S(2)}, u32[]{:S(2)}) async-start(f32[32,4,1280]{2,1,0:T(4,128)} %spectral.1), calls=%async_computation.1 | async-start | bytes 1310720 | tf_op jit(solution)/shard_map/all_to_all | solution.py:767
  45.3 0.0 copy-done.4
  45.3 3.7 %collective-permute-start.1 = (f32[1,4,32,128]{3,2,1,0:T(8,128)S(1)}, f32[1,4,32,128]{3,2,1,0:T(8,128)S(1)}, u32[]{:S(2)}, u32[]{:S(2)}) collective-permute-start(f32[1,4,32,128]{3,2,1,0:T(8,128)S(1)} %bitcast.13), channel_id=1, source_target_pairs={{0,3},{1,0},{2,1},{3,2},{4,7},{5,4},{6,5},{7,6},{8,11},{9,8},{10,9... | collective-permute-start | bytes 196616 | tf_op jit(solution)/shard_map/ppermute | solution.py:705
  49.0 0.0 collective-permute-start
  49.0 9.3 %collective-permute-done.1 = f32[1,4,32,128]{3,2,1,0:T(8,128)S(1)} collective-permute-done((f32[1,4,32,128]{3,2,1,0:T(8,128)S(1)}, f32[1,4,32,128]{3,2,1,0:T(8,128)S(1)}, u32[]{:S(2)}, u32[]{:S(2)}) %collective-permute-start.1) | collective-permute-done | bytes 65568 | tf_op jit(solution)/shard_map/ppermute | solution.py:705
  58.3 5.0 %collective-permute-done = f32[1,4,32,128]{3,2,1,0:T(8,128)S(1)} collective-permute-done((f32[1,4,32,128]{3,2,1,0:T(8,128)S(1)}, f32[1,4,32,128]{3,2,1,0:T(8,128)S(1)}, u32[]{:S(2)}, u32[]{:S(2)}) %collective-permute-start) | collective-permute-done | bytes 65568 | tf_op jit(solution)/shard_map/ppermute | solution.py:704
  63.4 0.1 collective-permute-start.2
  63.4 1.7 %collective-permute-start.3 = (f32[3,4,32,128]{3,2,1,0:T(8,128)S(1)}, f32[3,4,32,128]{3,2,1,0:T(8,128)S(1)}, u32[]{:S(2)}, u32[]{:S(2)}) collective-permute-start(f32[3,4,32,128]{3,2,1,0:T(8,128)S(1)} %pad_maximum_fusion), channel_id=1, source_target_pairs={{0,12},{4,0},{8,4},{12,8},{1,13},{5,1},{9,5},{13,9},{2,14},{6,2},{... | collective-permute-start | bytes 589832 | tf_op jit(solution)/shard_map/ppermute | solution.py:705
  65.2 3.7 %collective-permute-done.2 = f32[3,4,32,128]{3,2,1,0:T(8,128)S(1)} collective-permute-done((f32[3,4,32,128]{3,2,1,0:T(8,128)S(1)}, f32[3,4,32,128]{3,2,1,0:T(8,128)S(1)}, u32[]{:S(2)}, u32[]{:S(2)}) %collective-permute-start.2) | collective-permute-done | bytes 196640 | tf_op jit(solution)/shard_map/ppermute | solution.py:704
  68.9 0.8 collective-permute-done.3
  69.6 10.2 %pairs.1 = f32[3,32,128]{2,1,0:T(8,128)} custom-call(s32[64]{0:T(128)} %bitcast.19, s32[64]{0:T(128)} %bitcast.20, s32[5]{0:T(128)} %stack.23.refs_2_.refs_0_, f32[9,4,32,128]{3,2,1,0:T(8,128)S(1)} %constant_dynamic-update-slice_fusion.refs_3_), custom_call_target="tpu_custom_call" | custom-call | tf_op jit(solution)/shard_map/pairs/pallas_call | solution.py:798
  79.8 0.0 all-to-all-done.1.refs_2_
  79.9 16.3 %interpolate.1 = f32[3,32,128]{2,1,0:T(8,128)} custom-call(s32[5]{0:T(128)} %stack.23.refs_2_.refs_0_, f32[128,128]{1,0:T(8,128)} %constant.33.clone.refs_1_.refs_2_, f32[32,4,1280]{2,1,0:T(4,128)S(1)} %all-to-all-done.1.refs_2_, f32[4,32,128]{2,1,0:T(8,128)} %bitcast.12), custom_call_target="tpu_custom_call" | custom-call | tf_op jit(solution)/shard_map/interpolate/pallas_call | solution.py:816
  (6 shorter events, 0.1 us)
Async XLA Ops:
  12.2 25.2 %copy-start = (f32[128,128]{1,0:T(8,128)S(1)}, f32[128,128]{1,0:T(8,128)}, u32[]{:S(2)}) copy-start(f32[128,128]{1,0:T(8,128)} %constant.36.clone.refs_4_) | copy-start | bytes 196612
  12.2 25.2 %copy-start.1 = (f32[128,128]{1,0:T(8,128)S(1)}, f32[128,128]{1,0:T(8,128)}, u32[]{:S(2)}) copy-start(f32[128,128]{1,0:T(8,128)} %constant.35.clone.refs_3_) | copy-start | bytes 196612
  12.2 25.1 %copy-start.2 = (f32[128,128]{1,0:T(8,128)S(1)}, f32[128,128]{1,0:T(8,128)}, u32[]{:S(2)}) copy-start(f32[128,128]{1,0:T(8,128)} %constant.32.clone.refs_6_) | copy-start | bytes 196612
  12.2 25.1 %copy-start.3 = (f32[128,128]{1,0:T(8,128)S(1)}, f32[128,128]{1,0:T(8,128)}, u32[]{:S(2)}) copy-start(f32[128,128]{1,0:T(8,128)} %constant.31.clone.refs_5_) | copy-start | bytes 196612
  41.9 3.4 %copy-start.4 = (f32[4,1,1,4096]{3,2,1,0:T(1,128)S(1)}, f32[4,1,1,4096]{3,2,1,0:T(1,128)}, u32[]{:S(2)}) copy-start(f32[4,1,1,4096]{3,2,1,0:T(1,128)} %param.9) | copy-start | bytes 196612
  41.9 38.0 %all-to-all-start.1 = ((f32[32,4,1280]{2,1,0:T(4,128)}), f32[32,4,1280]{2,1,0:T(4,128)S(1)}, u32[]{:S(2)}, u32[]{:S(2)}) async-start(f32[32,4,1280]{2,1,0:T(4,128)} %spectral.1), calls=%async_computation.1 | async-start | bytes 1310720 | tf_op jit(solution)/shard_map/all_to_all | solution.py:767
  45.3 13.0 %collective-permute-start.1 = (f32[1,4,32,128]{3,2,1,0:T(8,128)S(1)}, f32[1,4,32,128]{3,2,1,0:T(8,128)S(1)}, u32[]{:S(2)}, u32[]{:S(2)}) collective-permute-start(f32[1,4,32,128]{3,2,1,0:T(8,128)S(1)} %bitcast.13), channel_id=1, source_target_pairs={{0,3},{1,0},{2,1},{3,2},{4,7},{5,4},{6,5},{7,6},{8,11},{9,8},{10,9... | collective-permute-start | bytes 196616 | tf_op jit(solution)/shard_map/ppermute | solution.py:705
  49.0 14.3 %collective-permute-start = (f32[1,4,32,128]{3,2,1,0:T(8,128)S(1)}, f32[1,4,32,128]{3,2,1,0:T(8,128)S(1)}, u32[]{:S(2)}, u32[]{:S(2)}) collective-permute-start(f32[1,4,32,128]{3,2,1,0:T(8,128)S(1)} %bitcast.14), channel_id=1, source_target_pairs={{0,1},{1,2},{2,3},{3,0},{4,5},{5,6},{6,7},{7,4},{8,9},{9,10},{10,1... | collective-permute-start | bytes 196616 | tf_op jit(solution)/shard_map/ppermute | solution.py:704
  63.4 5.5 %collective-permute-start.2 = (f32[3,4,32,128]{3,2,1,0:T(8,128)S(1)}, f32[3,4,32,128]{3,2,1,0:T(8,128)S(1)}, u32[]{:S(2)}, u32[]{:S(2)}) collective-permute-start(f32[3,4,32,128]{3,2,1,0:T(8,128)S(1)} %pad_maximum_fusion), channel_id=1, source_target_pairs={{0,4},{4,8},{8,12},{12,0},{1,5},{5,9},{9,13},{13,1},{2,6},{6,10},{... | collective-permute-start | bytes 589832 | tf_op jit(solution)/shard_map/ppermute | solution.py:704
  63.4 6.2 %collective-permute-start.3 = (f32[3,4,32,128]{3,2,1,0:T(8,128)S(1)}, f32[3,4,32,128]{3,2,1,0:T(8,128)S(1)}, u32[]{:S(2)}, u32[]{:S(2)}) collective-permute-start(f32[3,4,32,128]{3,2,1,0:T(8,128)S(1)} %pad_maximum_fusion), channel_id=1, source_target_pairs={{0,12},{4,0},{8,4},{12,8},{1,13},{5,1},{9,5},{13,9},{2,14},{6,2},{... | collective-permute-start | bytes 589832 | tf_op jit(solution)/shard_map/ppermute | solution.py:705

commit v3 on v2

--- a/solution.py
+++ b/solution.py
@@ -388,7 +388,7 @@
 
 
 def spread_kernel(
-    place_ref, basis_ref, atoms_ref, out_ref, acc_ref, row_ref,
+    basis_ref, atoms_ref, out_ref, acc_ref, row_ref,
     high_a, low_a, z_a, high_b, low_b, z_b, *, sizes
 ):
     chunk_tiles = z_a.shape[1] // LANES
@@ -406,8 +406,8 @@
             floor_x, theta_x, _ = spline_parts(parts[0])
             floor_y, theta_y, _ = spline_parts(parts[1])
             floor_z, theta_z, _ = spline_parts(parts[2])
-            floor_x = floor_x - place_ref[0].astype(jnp.float32)
-            floor_y = floor_y - place_ref[1].astype(jnp.float32)
+            floor_x = floor_x - (lax.axis_index("dom") * sizes["slab"]).astype(jnp.float32)
+            floor_y = floor_y - (lax.axis_index("pen") * sizes["column"]).astype(jnp.float32)
             z_high, z_low = split_bf16(choose(z_place(floor_z, LANES), theta_z))
             z_ref[:NG, span] = z_high
             z_ref[NG:, span] = z_low
@@ -473,7 +473,7 @@
 
 
 def spectral_kernel(
-    place_ref, line_ref, basis_ref, mixed_ref, mixed_t_ref, plane_ref, plane_sq_ref,
+    line_ref, basis_ref, mixed_ref, mixed_t_ref, plane_ref, plane_sq_ref,
     in_ref, out_ref, sum_ref, work_ref, *, sizes
 ):
     block, share, stride = sizes["block"], sizes["share"], sizes["stride"]
@@ -521,13 +521,15 @@
         )
 
     work_ref[...] = dot(work_ref[...], basis_ref[...], (1, 1))
+    device = (lax.axis_index("pen") * groups + lax.axis_index("grp")) * domains
+    first_line = (device + lax.axis_index("dom")) * share
     for kz in range(share):
         picked = work_ref[pl.ds(kz, NG, stride=share), :]
         spectrum = dot(mixed_ref[...], picked)
-        at = place_ref[2] + kz
+        at = first_line + kz
         freq = jnp.where(at > NG // 2, at - NG // 2, at)
         square = plane_sq_ref[...] + (freq * freq).astype(jnp.float32)
-        factor = plane_ref[...] * line_ref[freq] / jnp.maximum(square, 1.0)
+        factor = plane_ref[...] * line_ref[pl.ds(freq, 1), :] / jnp.maximum(square, 1.0)
         factor = jnp.where(square > 0.5, factor, 0.0)
         work_ref[pl.ds(kz, NG, stride=share), :] = dot(mixed_t_ref[...], spectrum * factor)
     work_ref[...] = dot(work_ref[...], basis_ref[...])
@@ -557,7 +559,7 @@
 
 
 def interpolate_kernel(
-    place_ref, basis_ref, coef_ref, atoms_ref, out_ref, pot_ref, table_ref,
+    basis_ref, coef_ref, atoms_ref, out_ref, pot_ref, table_ref,
     along_a, weight_a, along_b, weight_b, *, sizes, scale
 ):
     lanes = along_a.shape[1] // 2
@@ -601,8 +603,8 @@
             parts = [atoms_ref[part, pl.ds(tile, 1), :] for part in (0, 1, 3)]
             floor_x, theta_x, slope_x = spline_parts(parts[0])
             floor_y, theta_y, slope_y = spline_parts(parts[1])
-            floor_x = floor_x - place_ref[0].astype(jnp.float32)
-            floor_y = floor_y - place_ref[1].astype(jnp.float32)
+            floor_x = floor_x - (lax.axis_index("dom") * sizes["slab"]).astype(jnp.float32)
+            floor_y = floor_y - (lax.axis_index("pen") * sizes["column"]).astype(jnp.float32)
             place = row_ids(stride + 4, LANES) - floor_x
             kept = 2 * (side * tiles + block)
             table_ref[kept, :, :] = choose(place, theta_x)
@@ -655,22 +657,24 @@
 
 
 def pair_kernel(
-    home_ref, other_ref, place_ref, near_ref, out_ref, *, factors, scale, domains, pencils, together
+    listed_ref, near_ref, out_ref, *, factors, scale, domains, pencils, together
 ):
     tiles = near_ref.shape[2]
+    pairs = listed_ref.shape[0] // 2
+    dom_at, pen_at = lax.axis_index("dom"), lax.axis_index("pen")
     out_ref[...] = jnp.zeros_like(out_ref)
 
     def wrapped(seen, count):
         return jnp.where(seen < 0, -1.0, jnp.where(seen >= count, 1.0, 0.0))
 
     def one_pair(n):
-        home = home_ref[n]
-        other = other_ref[n]
+        home = listed_ref[n]
+        other = listed_ref[pairs + n]
         around = other // tiles
         tile = other - around * tiles
         step_dom = around // 3
-        wrap_x = wrapped(place_ref[3] + step_dom - 1, domains)
-        wrap_y = wrapped(place_ref[4] + around - 3 * step_dom - 1, pencils)
+        wrap_x = wrapped(dom_at + step_dom - 1, domains)
+        wrap_y = wrapped(pen_at + around - 3 * step_dom - 1, pencils)
         mine = [near_ref[4, part, pl.ds(home, 1), :] for part in range(4)]
         theirs = jnp.concatenate(
             [near_ref[around, part, pl.ds(tile, 1), :] for part in range(4)] * 2, axis=0
@@ -692,7 +696,7 @@
                 out_ref[axis, pl.ds(home, 1), :] += pushes[axis]
         return carry
 
-    lax.fori_loop(0, home_ref.shape[0] // together, some_pairs, 0)
+    lax.fori_loop(0, pairs // together, some_pairs, 0)
 
 
 def neighbours(block):
@@ -722,16 +726,11 @@
 def fast_on_device(atoms, pair_home, pair_other, *, sizes):
     groups, domains, pencils = sizes["groups"], sizes["domains"], sizes["pencils"]
     rows, share, block = sizes["rows"], sizes["share"], sizes["block"]
-    slab, column, stride = sizes["slab"], sizes["column"], sizes["stride"]
+    slab, stride = sizes["slab"], sizes["stride"]
     devices = groups * domains * pencils
     atom_count = atoms.shape[3]
     tiles = atom_count // LANES
     own = atoms.reshape(4, tiles, LANES)
-    dom_at = lax.axis_index("dom")
-    pen_at = lax.axis_index("pen")
-    grp_at = lax.axis_index("grp")
-    line_at = ((pen_at * groups + grp_at) * domains + dom_at) * share
-    place = jnp.stack([dom_at * slab, pen_at * column, line_at, dom_at, pen_at]).astype(jnp.int32)
     freq, basis = real_basis()
     order = (np.arange(domains)[None, :] * slab + np.arange(slab)[:, None]).reshape(-1)
     mixed = np.ascontiguousarray(basis[:, order])
@@ -739,6 +738,9 @@
     plane = in_vmem((line[:, None] * line[None, :] / np.pi).astype(np.float32))
     plane_sq = in_vmem((freq[:, None] ** 2 + freq[None, :] ** 2).astype(np.float32))
     basis_arr = jnp.asarray(basis)
+    kept_basis = in_vmem(basis)
+    line_rows = np.zeros((-(-(NG // 2 + 1) // SUBLANES) * SUBLANES, LANES), np.float32)
+    line_rows[: NG // 2 + 1] = line[: NG // 2 + 1, None]
     message = pltpu.VMEM((devices, share, rows), jnp.float32)
 
     nearby = in_vmem(neighbours(own))
@@ -746,7 +748,7 @@
     chunk = 512
     charge = pl.pallas_call(
         lambda *refs: spread_kernel(*refs, sizes=sizes),
-        in_specs=[smem_spec(), whole_spec(), whole_spec()],
+        in_specs=[whole_spec(), whole_spec()],
         out_specs=whole_spec(),
         out_shape=message,
         scratch_shapes=[
@@ -761,7 +763,7 @@
         * 2,
         grid=(),
         name="spread",
-    )(place, basis_arr, own)
+    )(basis_arr, own)
 
     def exchange(value):
         value = lax.all_to_all(value, MESH_AXES, split_axis=0, concat_axis=0, tiled=True)
@@ -770,7 +772,7 @@
     received = exchange(charge)
     returned = pl.pallas_call(
         lambda *refs: spectral_kernel(*refs, sizes=sizes),
-        in_specs=[smem_spec(), smem_spec()]
+        in_specs=[whole_spec()]
         + [whole_spec()] * 5
         + [whole_spec()],
         out_specs=whole_spec(),
@@ -782,9 +784,8 @@
         grid=(),
         name="spectral",
     )(
-        place,
-        jnp.asarray(line[: NG // 2 + 1].astype(np.float32)),
-        basis_arr,
+        in_vmem(line_rows),
+        kept_basis,
         in_vmem(mixed),
         in_vmem(mixed.T),
         plane,
@@ -804,18 +805,18 @@
             pencils=pencils,
             together=math.gcd(4, pairs),
         ),
-        in_specs=[smem_spec(), smem_spec(), smem_spec(), whole_spec()],
+        in_specs=[smem_spec(), whole_spec()],
         out_specs=whole_spec(),
         out_shape=out_shape,
         grid=(),
         name="pairs",
-    )(pair_home.reshape(-1), pair_other.reshape(-1), place, nearby)
+    )(jnp.concatenate([pair_home.reshape(-1), pair_other.reshape(-1)]), nearby)
 
     chunk = 256
     long_scale = -0.4 * NG / math.sqrt(NG * atom_count * devices)
     long_out = pl.pallas_call(
         lambda *refs: interpolate_kernel(*refs, sizes=sizes, scale=long_scale),
-        in_specs=[smem_spec(), whole_spec(), whole_spec(), whole_spec()],
+        in_specs=[whole_spec(), whole_spec(), whole_spec()],
         out_specs=whole_spec(),
         out_shape=out_shape,
         scratch_shapes=[
@@ -829,7 +830,7 @@
         * 2,
         grid=(),
         name="interpolate",
-    )(place, basis_arr, coefs, own)
+    )(kept_basis, coefs, in_vmem(own))
     return (short_out.reshape(3, 1, 1, atom_count), long_out.reshape(3, 1, 1, atom_count))
 
 

time: 97.6 us -> 96.1 us (0.985)
  the two profiles are of different devices: /device:TPU:0 before, /device:TPU:9 now
where the time goes in v3:
time: 96.1 us; the launch traced here: 95.8 us
  Pallas kernels  40.2 us (42%)
  blocking collectives  23.4 us (24%)
  waiting for transfers between devices  22.3 us (23%)
  starting transfers between devices  7.78 us (8%)
    all_to_all x1, blocking collectives, exchange(): lax.all_to_all(value, MESH_AXES, split_axis=0, concat_axis=0, tiled=True)  23.4 us
    ppermute x2, waiting for transfers between devices, neighbours(): lower = lax.ppermute(near, axis, up)  16.9 us
    pallas_call x1, Pallas kernels, fast_on_device(): pl.pallas_call(lambda *refs: interpolate_kernel(*refs, sizes=sizes, scale...  15.4 us
    pallas_call x1, Pallas kernels, fast_on_device(): pl.pallas_call(lambda *refs: spread_kernel(*refs, sizes=sizes), in_specs=...  10.8 us
    pallas_call x1, Pallas kernels, fast_on_device(): pl.pallas_call(lambda *refs: pair_kernel(*refs, factors=(2.0 * domains, 2...  10.3 us
    ppermute x2, waiting for transfers between devices, neighbours(): upper = lax.ppermute(near, axis, down)  5.41 us
    all_to_all x1, starting transfers between devices, exchange(): lax.all_to_all(value, MESH_AXES, split_axis=0, concat_axis=0, tiled=True)  4.15 us
    pallas_call x1, Pallas kernels, fast_on_device(): pl.pallas_call(lambda *refs: spectral_kernel(*refs, sizes=sizes), in_spec...  3.65 us
  transfers between devices with their start and end apart: 5, of which 4 were waited for; matrix products, arithmetic and copies ran while one was open for 1% of the time, Pallas kernels for 11%

profile of v3, /device:TPU:9, one launch (start us, length us, event | category | flops | bytes accessed | tf_op | source)
XLA Modules:
  0.0 95.8 jit_solution(14033800702516528685)
XLA Ops:
  0.6 10.8 %spread.1 = f32[32,4,1280]{2,1,0:T(4,128)S(1)} custom-call(f32[128,128]{1,0:T(8,128)} %constant.14.clone.refs_0_.refs_1_, f32[4,32,128]{2,1,0:T(8,128)} %bitcast.6), custom_call_target="tpu_custom_call" | custom-call | tf_op jit(solution)/shard_map/spread/pallas_call | solution.py:749
  11.5 0.0 copy-start.1
  11.5 0.0 copy-start.2
  11.5 0.0 copy-start.3
  11.5 0.0 copy-start.4
  11.5 0.0 copy-start.5
  11.5 0.0 copy-start.6
  11.6 23.4 %all_to_all.10.refs_6_ = f32[32,4,1280]{2,1,0:T(4,128)S(1)} all-to-all(f32[32,4,1280]{2,1,0:T(4,128)S(1)} %spread.1), channel_id=1, replica_groups=mesh['grp'=2,'dom'=4,'pen'=4] {'pen','grp','dom'}, dimensions={0} | all-to-all | bytes 1310720 | tf_op jit(solution)/shard_map/all_to_all | solution.py:769
  34.9 0.0 copy-done.1
  34.9 0.0 copy-done.2
  34.9 0.0 copy-done.3
  35.0 0.0 copy-done.4
  35.0 0.0 copy-done.5
  35.0 0.0 copy-done.6
  35.0 3.7 %spectral.1 = f32[32,4,1280]{2,1,0:T(4,128)} custom-call(f32[72,128]{1,0:T(8,128)S(1)} %copy-done.6, f32[128,128]{1,0:T(8,128)S(1)} %copy-done.1, f32[128,128]{1,0:T(8,128)S(1)} %copy-done.4, f32[128,128]{1,0:T(8,128)S(1)} %copy-done.5, f32[128,128]{1,0:T(8,128)S(1)} %copy-done.2, f32[128,128]{1,0:T(8,128)S(1)} %copy-done.3, ...), custom_call_target="tpu_custom_call" | custom-call | tf_op jit(solution)/shard_map/spectral/pallas_call | solution.py:773
  38.6 0.0 copy-start
  38.6 4.1 %all-to-all-start.1 = ((f32[32,4,1280]{2,1,0:T(4,128)}), f32[32,4,1280]{2,1,0:T(4,128)S(1)}, u32[]{:S(2)}, u32[]{:S(2)}) async-start(f32[32,4,1280]{2,1,0:T(4,128)} %spectral.1), calls=%async_computation.1 | async-start | bytes 1310720 | tf_op jit(solution)/shard_map/all_to_all | solution.py:769
  42.8 0.0 copy-done
  42.8 1.2 %collective-permute-start = (f32[1,4,32,128]{3,2,1,0:T(8,128)S(1)}, f32[1,4,32,128]{3,2,1,0:T(8,128)S(1)}, u32[]{:S(2)}, u32[]{:S(2)}) collective-permute-start(f32[1,4,32,128]{3,2,1,0:T(8,128)S(1)} %bitcast.7), channel_id=1, source_target_pairs={{0,1},{1,2},{2,3},{3,0},{4,5},{5,6},{6,7},{7,4},{8,9},{9,10},{10,1... | collective-permute-start | bytes 196616 | tf_op jit(solution)/shard_map/ppermute | solution.py:708
  44.0 0.3 collective-permute-start.1
  44.3 15.5 %collective-permute-done = f32[1,4,32,128]{3,2,1,0:T(8,128)S(1)} collective-permute-done((f32[1,4,32,128]{3,2,1,0:T(8,128)S(1)}, f32[1,4,32,128]{3,2,1,0:T(8,128)S(1)}, u32[]{:S(2)}, u32[]{:S(2)}) %collective-permute-start) | collective-permute-done | bytes 65568 | tf_op jit(solution)/shard_map/ppermute | solution.py:708
  59.9 1.7 %collective-permute-done.1 = f32[1,4,32,128]{3,2,1,0:T(8,128)S(1)} collective-permute-done((f32[1,4,32,128]{3,2,1,0:T(8,128)S(1)}, f32[1,4,32,128]{3,2,1,0:T(8,128)S(1)}, u32[]{:S(2)}, u32[]{:S(2)}) %collective-permute-start.1) | collective-permute-done | bytes 65568 | tf_op jit(solution)/shard_map/ppermute | solution.py:709
  61.6 2.1 %collective-permute-start.2 = (f32[3,4,32,128]{3,2,1,0:T(8,128)S(1)}, f32[3,4,32,128]{3,2,1,0:T(8,128)S(1)}, u32[]{:S(2)}, u32[]{:S(2)}) collective-permute-start(f32[3,4,32,128]{3,2,1,0:T(8,128)S(1)} %pad_maximum_fusion), channel_id=1, source_target_pairs={{0,4},{4,8},{8,12},{12,0},{1,5},{5,9},{9,13},{13,1},{2,6},{6,10},{... | collective-permute-start | bytes 589832 | tf_op jit(solution)/shard_map/ppermute | solution.py:708
  63.7 0.0 copy-start.7
  63.7 0.0 copy-start.8
  63.7 0.7 copy-done.7
  64.4 0.0 copy-done.8
  64.4 0.6 pad_add_fusion.refs_0_
  65.0 0.0 collective-permute-start.3
  65.0 1.4 %collective-permute-done.2 = f32[3,4,32,128]{3,2,1,0:T(8,128)S(1)} collective-permute-done((f32[3,4,32,128]{3,2,1,0:T(8,128)S(1)}, f32[3,4,32,128]{3,2,1,0:T(8,128)S(1)}, u32[]{:S(2)}, u32[]{:S(2)}) %collective-permute-start.2) | collective-permute-done | bytes 196640 | tf_op jit(solution)/shard_map/ppermute | solution.py:708
  66.4 3.7 %collective-permute-done.3 = f32[3,4,32,128]{3,2,1,0:T(8,128)S(1)} collective-permute-done((f32[3,4,32,128]{3,2,1,0:T(8,128)S(1)}, f32[3,4,32,128]{3,2,1,0:T(8,128)S(1)}, u32[]{:S(2)}, u32[]{:S(2)}) %collective-permute-start.3) | collective-permute-done | bytes 196640 | tf_op jit(solution)/shard_map/ppermute | solution.py:709
  70.1 10.3 %pairs.1 = f32[3,32,128]{2,1,0:T(8,128)} custom-call(s32[128]{0:T(128)} %pad_add_fusion.refs_0_, f32[9,4,32,128]{3,2,1,0:T(8,128)S(1)} %constant_dynamic-update-slice_fusion.refs_1_), custom_call_target="tpu_custom_call" | custom-call | tf_op jit(solution)/shard_map/pairs/pallas_call | solution.py:799
  80.4 0.0 all-to-all-done.1.refs_1_
  80.4 15.4 %interpolate.1 = f32[3,32,128]{2,1,0:T(8,128)} custom-call(f32[128,128]{1,0:T(8,128)S(1)} %copy-done.1, f32[32,4,1280]{2,1,0:T(4,128)S(1)} %all-to-all-done.1.refs_1_, f32[4,32,128]{2,1,0:T(8,128)S(1)} %bitcast.11), custom_call_target="tpu_custom_call" | custom-call | tf_op jit(solution)/shard_map/interpolate/pallas_call | solution.py:817
  (6 shorter events, 0.1 us)
Async XLA Ops:
  11.5 23.5 %copy-start.1 = (f32[128,128]{1,0:T(8,128)S(1)}, f32[128,128]{1,0:T(8,128)}, u32[]{:S(2)}) copy-start(f32[128,128]{1,0:T(8,128)} %constant.14.clone.refs_0_.refs_1_) | copy-start | bytes 196612
  11.5 23.5 %copy-start.2 = (f32[128,128]{1,0:T(8,128)S(1)}, f32[128,128]{1,0:T(8,128)}, u32[]{:S(2)}) copy-start(f32[128,128]{1,0:T(8,128)} %constant.12.clone.refs_4_) | copy-start | bytes 196612
  11.5 23.4 %copy-start.3 = (f32[128,128]{1,0:T(8,128)S(1)}, f32[128,128]{1,0:T(8,128)}, u32[]{:S(2)}) copy-start(f32[128,128]{1,0:T(8,128)} %constant.13.clone.refs_5_) | copy-start | bytes 196612
  11.5 23.4 %copy-start.4 = (f32[128,128]{1,0:T(8,128)S(1)}, f32[128,128]{1,0:T(8,128)}, u32[]{:S(2)}) copy-start(f32[128,128]{1,0:T(8,128)} %constant.16.clone.refs_2_) | copy-start | bytes 196612
  11.5 23.4 %copy-start.5 = (f32[128,128]{1,0:T(8,128)S(1)}, f32[128,128]{1,0:T(8,128)}, u32[]{:S(2)}) copy-start(f32[128,128]{1,0:T(8,128)} %constant.17.clone.refs_3_) | copy-start | bytes 196612
  11.5 23.4 %copy-start.6 = (f32[72,128]{1,0:T(8,128)S(1)}, f32[72,128]{1,0:T(8,128)}, u32[]{:S(2)}) copy-start(f32[72,128]{1,0:T(8,128)} %constant.15.clone.refs_0_) | copy-start | bytes 110596
  38.6 4.2 %copy-start = (f32[4,1,1,4096]{3,2,1,0:T(1,128)S(1)}, f32[4,1,1,4096]{3,2,1,0:T(1,128)}, u32[]{:S(2)}) copy-start(f32[4,1,1,4096]{3,2,1,0:T(1,128)} %param.9) | copy-start | bytes 196612
  38.6 41.7 %all-to-all-start.1 = ((f32[32,4,1280]{2,1,0:T(4,128)}), f32[32,4,1280]{2,1,0:T(4,128)S(1)}, u32[]{:S(2)}, u32[]{:S(2)}) async-start(f32[32,4,1280]{2,1,0:T(4,128)} %spectral.1), calls=%async_computation.1 | async-start | bytes 1310720 | tf_op jit(solution)/shard_map/all_to_all | solution.py:769
  42.8 17.1 %collective-permute-start = (f32[1,4,32,128]{3,2,1,0:T(8,128)S(1)}, f32[1,4,32,128]{3,2,1,0:T(8,128)S(1)}, u32[]{:S(2)}, u32[]{:S(2)}) collective-permute-start(f32[1,4,32,128]{3,2,1,0:T(8,128)S(1)} %bitcast.7), channel_id=1, source_target_pairs={{0,1},{1,2},{2,3},{3,0},{4,5},{5,6},{6,7},{7,4},{8,9},{9,10},{10,1... | collective-permute-start | bytes 196616 | tf_op jit(solution)/shard_map/ppermute | solution.py:708
  44.0 17.6 %collective-permute-start.1 = (f32[1,4,32,128]{3,2,1,0:T(8,128)S(1)}, f32[1,4,32,128]{3,2,1,0:T(8,128)S(1)}, u32[]{:S(2)}, u32[]{:S(2)}) collective-permute-start(f32[1,4,32,128]{3,2,1,0:T(8,128)S(1)} %bitcast.8), channel_id=1, source_target_pairs={{0,3},{1,0},{2,1},{3,2},{4,7},{5,4},{6,5},{7,6},{8,11},{9,8},{10,9... | collective-permute-start | bytes 196616 | tf_op jit(solution)/shard_map/ppermute | solution.py:709
  61.6 4.7 %collective-permute-start.2 = (f32[3,4,32,128]{3,2,1,0:T(8,128)S(1)}, f32[3,4,32,128]{3,2,1,0:T(8,128)S(1)}, u32[]{:S(2)}, u32[]{:S(2)}) collective-permute-start(f32[3,4,32,128]{3,2,1,0:T(8,128)S(1)} %pad_maximum_fusion), channel_id=1, source_target_pairs={{0,4},{4,8},{8,12},{12,0},{1,5},{5,9},{9,13},{13,1},{2,6},{6,10},{... | collective-permute-start | bytes 589832 | tf_op jit(solution)/shard_map/ppermute | solution.py:708
  63.7 0.7 copy-start.7
  63.7 0.7 copy-start.8
  65.0 5.1 %collective-permute-start.3 = (f32[3,4,32,128]{3,2,1,0:T(8,128)S(1)}, f32[3,4,32,128]{3,2,1,0:T(8,128)S(1)}, u32[]{:S(2)}, u32[]{:S(2)}) collective-permute-start(f32[3,4,32,128]{3,2,1,0:T(8,128)S(1)} %pad_maximum_fusion), channel_id=1, source_target_pairs={{0,12},{4,0},{8,4},{12,8},{1,13},{5,1},{9,5},{13,9},{2,14},{6,2},{... | collective-permute-start | bytes 589832 | tf_op jit(solution)/shard_map/ppermute | solution.py:709
